TPU v7x, 64 devices: a 2x2x8 block of a 4x4x8 slice. The times are simulated.
64 devices in a mesh: dp: 4 (over x, y), ep: 16 (over z, core).
Axes of the slice: x: 2, y: 2, z: 8, core: 2. Of those that a mesh axis runs over, the one named last changes fastest.
The devices are a block of a 4x4x8 slice.
Arguments:
- hidden_in: bfloat16 [6144, 2048], P(('dp', 'ep')), parts along dimension 0
- norm_gain: float32 [2048], replicated
- router_w: float32 [64, 2048], replicated
- w_gate: bfloat16 [64, 2048, 1408], P('ep')
- w_up: bfloat16 [64, 2048, 1408], P('ep')
- w_down: bfloat16 [64, 1408, 2048], P('ep')
- ws_gate: bfloat16 [2048, 2816], replicated
- ws_up: bfloat16 [2048, 2816], replicated
- ws_down: bfloat16 [2816, 2048], replicated
- expert_ids: int32 [6144, 6], P(('dp', 'ep')), parts along dimension 0
Outputs:
- output: bfloat16 [6144, 2048], P(('dp', 'ep')), parts along dimension 0
There are 4 independent parts. A program takes and returns all parts, laid end to end along the dimension named above; an argument that names none is the same for every part.
All inputs are finite; a program needn't handle non-finite values.
Results may differ from a plain program's by a relative error of at most 0.00428517.
Values are sent between devices in bfloat16 or wider.
A program may use at most 768 MiB of HBM per device.

v0:
```python
import jax
import jax.numpy as jnp
from jax import lax
from jax.sharding import PartitionSpec as P

NORM_EPS = 1e-6
ROUTE_SCALE = 2.5
GROUPS = 8
GROUP_LIMIT = 4


def rms_norm(x_rows, norm_gain):
    x_f32 = x_rows.astype(jnp.float32)
    inv_rms = lax.rsqrt(jnp.mean(x_f32 * x_f32, axis=-1, keepdims=True) + NORM_EPS)
    return (x_f32 * inv_rms * norm_gain).astype(jnp.bfloat16)


def route_gates(x_norm, router_w, expert_ids):
    logits = jnp.einsum("td,nd->tn", x_norm.astype(jnp.float32), router_w, precision=lax.Precision.HIGHEST, preferred_element_type=jnp.float32)
    picked = jnp.take_along_axis(jax.nn.sigmoid(logits), expert_ids, axis=1)
    return ROUTE_SCALE * picked / jnp.sum(picked, axis=1, keepdims=True)


def swiglu(tok_rows, gate_mat, up_mat, down_mat):
    h_gate = jnp.dot(tok_rows, gate_mat, preferred_element_type=jnp.float32)
    h_up = jnp.dot(tok_rows, up_mat, preferred_element_type=jnp.float32)
    hidden = (jax.nn.silu(h_gate) * h_up).astype(jnp.bfloat16)
    return jnp.dot(hidden, down_mat, preferred_element_type=jnp.float32).astype(jnp.bfloat16)


def expert_stack(expert_in, w_gate, w_up, w_down):
    h_gate = jnp.einsum("ecd,edi->eci", expert_in, w_gate, preferred_element_type=jnp.float32)
    h_up = jnp.einsum("ecd,edi->eci", expert_in, w_up, preferred_element_type=jnp.float32)
    hidden = (jax.nn.silu(h_gate) * h_up).astype(jnp.bfloat16)
    return jnp.einsum("eci,eid->ecd", hidden, w_down, preferred_element_type=jnp.float32).astype(jnp.bfloat16)


def solution(mesh):
    ep_size = mesh.shape["ep"]

    def local_block(hidden_in, norm_gain, router_w, w_gate, w_up, w_down, ws_gate, ws_up, ws_down, expert_ids):
        tok_dev, top_k = expert_ids.shape
        model_dim = hidden_in.shape[1]
        exp_dev = w_gate.shape[0]
        pair_cap = GROUPS * ((top_k + GROUP_LIMIT - 1) // GROUP_LIMIT) * tok_dev // ep_size
        recv_cap = pair_cap * ep_size
        exp_cap = recv_cap // exp_dev
        x_norm = rms_norm(hidden_in, norm_gain)
        gate_vals = route_gates(x_norm, router_w, expert_ids)
        shared_out = swiglu(x_norm, ws_gate, ws_up, ws_down)

        flat_ids = expert_ids.reshape(-1)
        dest_dev = flat_ids // exp_dev
        dest_hot = (dest_dev[:, None] == jnp.arange(ep_size, dtype=jnp.int32)[None, :]).astype(jnp.int32)
        dest_rank = jnp.sum((jnp.cumsum(dest_hot, axis=0) - 1) * dest_hot, axis=1)
        send_slot = dest_dev * pair_cap + dest_rank
        pair_tok = jnp.arange(tok_dev * top_k, dtype=jnp.int32) // top_k
        slot_tok = jnp.full((recv_cap,), tok_dev, jnp.int32).at[send_slot].set(pair_tok)
        slot_exp = jnp.full((recv_cap,), -1, jnp.int32).at[send_slot].set(flat_ids % exp_dev)
        send_rows = jnp.take(x_norm, slot_tok, axis=0, mode="fill", fill_value=0)
        recv_rows = lax.all_to_all(send_rows, "ep", 0, 0, tiled=True)
        recv_exp = lax.all_to_all(slot_exp, "ep", 0, 0, tiled=True)

        exp_hot = (recv_exp[:, None] == jnp.arange(exp_dev, dtype=jnp.int32)[None, :]).astype(jnp.int32)
        exp_rank = jnp.sum((jnp.cumsum(exp_hot, axis=0) - 1) * exp_hot, axis=1)
        buf_slot = jnp.where(recv_exp >= 0, recv_exp * exp_cap + exp_rank, recv_cap)
        buf_row = jnp.full((recv_cap,), recv_cap, jnp.int32).at[buf_slot].set(jnp.arange(recv_cap, dtype=jnp.int32), mode="drop")
        expert_in = jnp.take(recv_rows, buf_row, axis=0, mode="fill", fill_value=0).reshape(exp_dev, exp_cap, model_dim)
        expert_out = expert_stack(expert_in, w_gate, w_up, w_down).reshape(recv_cap, model_dim)
        back_rows = jnp.take(expert_out, buf_slot, axis=0, mode="fill", fill_value=0)
        returned = lax.all_to_all(back_rows, "ep", 0, 0, tiled=True)

        pair_out = jnp.take(returned, send_slot, axis=0).reshape(tok_dev, top_k, model_dim)
        routed = jnp.sum(gate_vals[:, :, None] * pair_out.astype(jnp.float32), axis=1)
        return (hidden_in.astype(jnp.float32) + shared_out.astype(jnp.float32) + routed).astype(jnp.bfloat16)

    row_spec = P(("dp", "ep"), None)
    in_specs = (row_spec, P(), P(), P("ep"), P("ep"), P("ep"), P(), P(), P(), row_spec)
    return jax.shard_map(local_block, mesh=mesh, in_specs=in_specs, out_specs=row_spec, check_vma=False)
```

profile of v0, /device:TPU:22, one launch (start us, length us, event | category | flops | bytes accessed | tf_op | source)
XLA Modules:
  0.0 457.0 jit_solution(284875006446281636)
XLA Ops:
  0.0 0.0 copy-start
  0.0 0.8 copy.49
  0.8 0.1 reshape.249
  1.0 0.1 reshape.252
  1.2 1.4 reduce-window.14
  2.6 0.2 slice_reduce_fusion
  2.9 0.1 bitcast_bitcast_fusion
  3.0 4.1 scatter_custom_fusion.1
  7.1 0.7 all_to_all.22
  7.8 9.6 %all-to-all-start.1 = ((s32[16,96,1]{1,2,0:T(1,128)}), s32[16,96,1]{1,2,0:T(1,128)S(1)}, u32[]{:S(2)}, u32[]{:S(2)}) async-start(s32[16,96,1]{1,2,0:T(1,128)} %all_to_all.22), calls=%async_computation.1 | async-start | bytes 16384 | tf_op jit(solution)/shard_map/all_to_all | solution.py:62
  17.4 4.1 scatter_custom_fusion
  21.6 1.2 fusion.8
  22.8 0.1 broadcast_in_dim.59
  22.9 1.2 fusion.10
  24.0 7.1 %gather_fusion = bf16[1536,2048]{1,0:T(8,128)(2,1)} fusion(bf16[96,2048]{1,0:T(8,128)(2,1)S(1)} %fusion.10, s32[2048]{0:T(1024)S(1)} %pad_clamp_fusion.2), kind=kCustom, calls=%fused_computation.2 | custom fusion | bytes 12589056 | tf_op jit(solution)/shard_map/jit(_take)/gather | solution.py:60
  31.1 5.9 %broadcast_select_fusion.2 = bf16[16,96,2048]{2,1,0:T(8,128)(2,1)} fusion(bf16[16,96,2048]{2,1,0:T(8,128)(2,1)} %bitcast.60, pred[16,96]{1,0:T(8,128)(4,1)S(1)} %broadcast_in_dim.59), kind=kLoop, calls=%fused_computation.12 | loop fusion | flops 3145728 | bytes 12584448 | tf_op jit(solution)/shard_map/jit(_take)/select_n | solution.py:60
  37.1 0.0 all-to-all-done.1
  37.1 7.2 %all-to-all-start = ((bf16[16,96,2048]{2,1,0:T(8,128)(2,1)}), bf16[16,96,2048]{2,1,0:T(8,128)(2,1)}, u32[]{:S(2)}, u32[]{:S(2)}) async-start(bf16[16,96,2048]{2,1,0:T(8,128)(2,1)} %broadcast_select_fusion.2), calls=%async_computation | async-start | bytes 12582912 | tf_op jit(solution)/shard_map/all_to_all | solution.py:61
  44.3 0.1 eq.57
  44.4 1.1 reduce-window.16
  45.5 0.2 slice_reduce_fusion.1
  45.8 0.2 reduce-window.19
  46.0 0.5 broadcast.352
  46.5 0.7 fusion.41
  47.2 0.1 eq.53
  47.2 0.1 mul.112
  47.4 0.1 ge.48
  47.4 0.1 add_bitcast_fusion.1
  47.6 6.4 %scatter_custom_fusion.2 = s32[1536]{0:T(1024)S(1)} fusion(s32[1536]{0:T(1024)S(1)} %fusion.17, s32[1536]{0:T(1024)S(1)} %iota.20, s32[]{:T(128)} %constant.121.clone.1), kind=kCustom, calls=%fused_computation.91 | custom fusion | bytes 6148 | tf_op jit(solution)/shard_map/scatter | solution.py:67
  54.1 131.1 %all-to-all-done = bf16[16,96,2048]{2,1,0:T(8,128)(2,1)} async-done(((bf16[16,96,2048]{2,1,0:T(8,128)(2,1)}), bf16[16,96,2048]{2,1,0:T(8,128)(2,1)}, u32[]{:S(2)}, u32[]{:S(2)}) %all-to-all-start) | async-done | bytes 6291488 | tf_op jit(solution)/shard_map/all_to_all | solution.py:61
  185.2 16.3 %gather_fusion.3 = bf16[1536,2048]{1,0:T(8,128)(2,1)} fusion(bf16[1536,2048]{1,0:T(8,128)(2,1)} %bitcast.4, s32[2048]{0:T(1024)S(1)} %pad_clamp_fusion.1), kind=kCustom, calls=%fused_computation.clone | custom fusion | bytes 12589056 | tf_op jit(solution)/shard_map/jit(_take)/gather | solution.py:68
  201.5 5.9 %broadcast_select_fusion.1 = bf16[1536,2048]{1,0:T(8,128)(2,1)} fusion(bf16[1536,2048]{1,0:T(8,128)(2,1)} %gather_fusion.3, pred[1536]{0:T(1024)(128)(4,1)S(1)} %compare_and_fusion.1), kind=kLoop, calls=%fused_computation.11 | loop fusion | flops 3145728 | bytes 12584448 | tf_op jit(solution)/shard_map/jit(_take)/select_n | solution.py:68
  207.3 18.6 %fusion.42 = f32[4,384,1408]{2,1,0:T(8,128)} fusion(bf16[4,384,2048]{2,1,0:T(8,128)(2,1)} %bitcast.61, bf16[4,2048,1408]{2,1,0:T(8,128)(2,1)} %param.15), kind=kOutput, calls=%fused_computation.110 | convolution fusion | flops 8858370048 | bytes 38010880 | tf_op jit(solution)/shard_map/ecd,edi->eci/dot_general | solution.py:32
  225.9 28.0 %convolution_convert_fusion = bf16[4,384,2048]{2,1,0:T(8,128)(2,1)} fusion(bf16[4,1408,2048]{2,1,0:T(8,128)(2,1)} %param.17, f32[4,384,1408]{2,1,0:T(8,128)} %fusion.42, bf16[4,384,2048]{2,1,0:T(8,128)(2,1)} %bitcast.62, bf16[4,2048,1408]{2,1,0:T(8,128)(2,1)} %param.16), kind=kOutput, calls=%fused_computation.13 | convolution fusion | flops 17732861952 | bytes 67371008 | tf_op jit(solution)/shard_map/eci,eid->ecd/dot_general | solution.py:35
  253.9 16.5 %gather_fusion.4 = bf16[1536,2048]{1,0:T(8,128)(2,1)} fusion(bf16[1536,2048]{1,0:T(8,128)(2,1)} %bitcast.58, s32[2048]{0:T(1024)S(1)} %pad_clamp_fusion), kind=kCustom, calls=%fused_computation.1.clone | custom fusion | bytes 12589056 | tf_op jit(solution)/shard_map/jit(_take)/gather | solution.py:70
  270.4 5.9 %broadcast_select_fusion = bf16[1536,2048]{1,0:T(8,128)(2,1)} fusion(bf16[1536,2048]{1,0:T(8,128)(2,1)} %gather_fusion.4, pred[1536]{0:T(1024)(128)(4,1)S(1)} %get-tuple-element.8), kind=kLoop, calls=%fused_computation.10 | loop fusion | flops 3145728 | bytes 12584448 | tf_op jit(solution)/shard_map/jit(_take)/select_n | solution.py:70
  276.3 0.0 copy-start.3
  276.3 0.0 copy-start.1
  276.3 0.0 copy-start.2
  276.3 9.4 %all-to-all-start.2 = ((bf16[16,96,2048]{2,1,0:T(8,128)(2,1)}), bf16[16,96,2048]{2,1,0:T(8,128)(2,1)}, u32[]{:S(2)}, u32[]{:S(2)}) async-start(bf16[16,96,2048]{2,1,0:T(8,128)(2,1)} %bitcast.59), calls=%async_computation.2 | async-start | bytes 12582912 | tf_op jit(solution)/shard_map/all_to_all | solution.py:71
  285.7 0.1 reduce_sum.54
  285.9 0.1 copy.52
  285.9 0.0 copy-done.3
  286.0 0.1 copy.53
  286.1 0.1 copy.46
  286.2 0.1 reshape.289
  286.3 0.0 copy-done
  286.3 0.0 copy-done.1
  286.4 0.0 copy-done.2
  286.4 0.6 fusion.7
  287.0 4.0 gather_fusion.2
  291.0 0.1 reshape.292
  291.2 0.1 copy.47
  291.3 0.1 copy.48
  291.4 7.3 %fusion.39 = f32[96,2816]{1,0:T(8,128)} fusion(bf16[2048,2816]{1,0:T(8,128)(2,1)} %param.18, bf16[96,2048]{1,0:T(8,128)(2,1)S(1)} %copy-done.1, f32[2048]{0:T(1024)S(1)} %copy-done.2, f32[96]{0:T(128)S(1)} %add_rsqrt_fusion), kind=kOutput, calls=%fused_computation.108 | convolution fusion | flops 1108082688 | bytes 13017472 | tf_op jit(solution)/shard_map/dot_general | solution.py:25
  298.7 127.8 %all-to-all-done.2 = bf16[16,96,2048]{2,1,0:T(8,128)(2,1)} async-done(((bf16[16,96,2048]{2,1,0:T(8,128)(2,1)}), bf16[16,96,2048]{2,1,0:T(8,128)(2,1)}, u32[]{:S(2)}, u32[]{:S(2)}) %all-to-all-start.2) | async-done | bytes 6291488 | tf_op jit(solution)/shard_map/all_to_all | solution.py:71
  426.6 9.9 %gather_fusion.1 = bf16[576,2048]{1,0:T(8,128)(2,1)S(1)} fusion(bf16[1536,2048]{1,0:T(8,128)(2,1)} %bitcast.8, s32[1024]{0:T(1024)S(1)} %pad_clamp_fusion.3), kind=kCustom, calls=%fused_computation.3 | custom fusion | bytes 4720896 | tf_op jit(solution)/shard_map/jit(_take)/gather | solution.py:73
  436.5 2.5 gather.23
  438.9 5.3 %multiply_reduce_fusion = f32[96,2048]{1,0:T(8,128)S(1)} fusion(bf16[96,6,2048]{2,1,0:T(8,128)(2,1)} %gather.23, f32[96,6]{1,0:T(8,128)S(1)} %copy.48, pred[96,6]{1,0:T(8,128)(4,1)S(1)} %copy.53), kind=kLoop, calls=%fused_computation.9 | loop fusion | flops 4521984 | bytes 3148608 | tf_op jit(solution)/shard_map/reduce_sum | solution.py:74
  444.3 12.7 %fusion.4 = bf16[96,2048]{1,0:T(8,128)(2,1)} fusion(f32[96,2048]{1,0:T(8,128)S(1)} %multiply_reduce_fusion, bf16[2816,2048]{1,0:T(8,128)(2,1)} %param.20, bf16[96,2048]{1,0:T(8,128)(2,1)S(1)} %copy-done.1, bf16[2048,2816]{1,0:T(8,128)(2,1)} %param.19, f32[96,2816]{1,0:T(8,128)} %fusion.39, f32[2048]{0:T(1024)S(1)} %copy-done.2, f32[96]{0:T(128)S(1)} %add_rsqrt_fusion), kind=kOutput, calls=%fused_computation.20 | convolution fusion | flops 2218180608 | bytes 25731456 | tf_op jit(solution)/shard_map/dot_general | solution.py:28
  (26 shorter events, 0.4 us)
Async XLA Ops:
  0.0 286.3 %copy-start = (f32[64,2048]{1,0:T(8,128)S(1)}, f32[64,2048]{1,0:T(8,128)}, u32[]{:S(2)}) copy-start(f32[64,2048]{1,0:T(8,128)} %param.14) | copy-start | bytes 1572868
  7.8 29.3 %all-to-all-start.1 = ((s32[16,96,1]{1,2,0:T(1,128)}), s32[16,96,1]{1,2,0:T(1,128)S(1)}, u32[]{:S(2)}, u32[]{:S(2)}) async-start(s32[16,96,1]{1,2,0:T(1,128)} %all_to_all.22), calls=%async_computation.1 | async-start | bytes 16384 | tf_op jit(solution)/shard_map/all_to_all | solution.py:62
  37.1 148.1 %all-to-all-start = ((bf16[16,96,2048]{2,1,0:T(8,128)(2,1)}), bf16[16,96,2048]{2,1,0:T(8,128)(2,1)}, u32[]{:S(2)}, u32[]{:S(2)}) async-start(bf16[16,96,2048]{2,1,0:T(8,128)(2,1)} %broadcast_select_fusion.2), calls=%async_computation | async-start | bytes 12582912 | tf_op jit(solution)/shard_map/all_to_all | solution.py:61
  276.3 9.6 %copy-start.3 = (s32[96,6]{0,1:T(8,128)S(1)}, s32[96,6]{0,1:T(8,128)}, u32[]{:S(2)}) copy-start(s32[96,6]{0,1:T(8,128)} %param.21) | copy-start | bytes 6916
  276.3 10.1 %copy-start.1 = (bf16[96,2048]{1,0:T(8,128)(2,1)S(1)}, bf16[96,2048]{1,0:T(8,128)(2,1)}, u32[]{:S(2)}) copy-start(bf16[96,2048]{1,0:T(8,128)(2,1)} %param.12) | copy-start | bytes 1179652
  276.3 10.1 %copy-start.2 = (f32[2048]{0:T(1024)S(1)}, f32[2048]{0:T(1024)}, u32[]{:S(2)}) copy-start(f32[2048]{0:T(1024)} %param.13) | copy-start | bytes 24580
  276.3 150.3 %all-to-all-start.2 = ((bf16[16,96,2048]{2,1,0:T(8,128)(2,1)}), bf16[16,96,2048]{2,1,0:T(8,128)(2,1)}, u32[]{:S(2)}, u32[]{:S(2)}) async-start(bf16[16,96,2048]{2,1,0:T(8,128)(2,1)} %bitcast.59), calls=%async_computation.2 | async-start | bytes 12582912 | tf_op jit(solution)/shard_map/all_to_all | solution.py:71
where the time goes:
time: 459 us; the launch traced here: 457 us
  waiting for transfers between devices  259 us (56%)
  local copies, waits for them, and re-layouts  75 us (16%)
  matrix products  67.2 us (15%)
  other arithmetic  29.3 us (6%)
  starting transfers between devices  26.2 us (6%)
    all_to_all x1, waiting for transfers between devices, local_block(): recv_rows = lax.all_to_all(send_rows, 'ep', 0, 0, tiled=True)  131 us
    all_to_all x1, waiting for transfers between devices, local_block(): returned = lax.all_to_all(back_rows, 'ep', 0, 0, tiled=True)  128 us
    dot_general x1, matrix products, expert_stack(): jnp.einsum('eci,eid->ecd', hidden, w_down, preferred_element_type=jnp.flo...  28 us
    dot_general x1, matrix products, expert_stack(): jnp.einsum('ecd,edi->eci', expert_in, w_gate, preferred_element_type=jnp....  18.6 us
    gather x1, local copies, waits for them, and re-layouts, local_block(): jnp.take(expert_out, buf_slot, axis=0, mode='fill', fill_value=0)  16.5 us
    gather x1, local copies, waits for them, and re-layouts, local_block(): jnp.take(recv_rows, buf_row, axis=0, mode='fill', fill_value=0)  16.3 us
    dot_general x1, matrix products, swiglu(): jnp.dot(hidden, down_mat, preferred_element_type=jnp.float32)  12.7 us
    gather x2, local copies, waits for them, and re-layouts, local_block(): jnp.take(returned, send_slot, axis=0).reshape(tok_dev, top_k, model_dim)  12.4 us
  transfers between devices with their start and end apart: 3, of which 2 were waited for; matrix products, arithmetic and copies ran while one was open for 9% of the time, Pallas kernels for 0%

commit v1 on v0

v1 whole, which is shorter than its diff:
```python
import functools

import jax
import jax.numpy as jnp
from jax import lax
from jax.experimental import pallas as pl
from jax.experimental.pallas import tpu as pltpu
from jax.sharding import PartitionSpec as P

NORM_EPS = 1e-6
ROUTE_SCALE = 2.5
GROUPS = 8
GROUP_LIMIT = 4
LANES = 128
COLS = 256
STREAM_SLOTS = 6
MESH = pl.DeviceIdType.MESH
F32 = jnp.float32
BF16 = jnp.bfloat16


def moe_kernel(
    ep_size,
    cap,
    hidden_ref,
    gain_ref,
    router_ref,
    ids_ref,
    wg_hbm,
    wu_hbm,
    wd_hbm,
    sg_hbm,
    su_hbm,
    sd_hbm,
    out_ref,
    xbuf,
    gsend,
    gmsg,
    rank_ref,
    cols_ref,
    pick,
    place,
    xg,
    hid,
    shid,
    sout,
    wbuf,
    dbuf,
    part,
    erows,
    from_core,
    ring,
    w_sem,
    d_sem,
    ag_send,
    ag_recv,
    cc_send,
    cc_recv,
    g_send,
    g_recv,
    p_send,
    p_recv,
    r_send,
    r_recv,
):
    tok, dim = hidden_ref.shape
    half = tok // 2
    top_k = ids_ref.shape[1]
    n_exp = wg_hbm.shape[0]
    inter = wg_hbm.shape[2]
    s_inter = sg_hbm.shape[1]
    chips = ep_size // 2
    far = chips // 2
    own_pos = chips - 2
    far_pos = chips - 1
    n_groups = chips // 2
    group_rows = 4 * tok
    tiles_per_group = group_rows // LANES
    n_chunks = dim // COLS
    slots = n_exp * cap
    sh_steps = s_inter // LANES
    ex_steps = inter // LANES
    w_steps = sh_steps + n_exp * ex_steps
    d_per = n_exp + 2

    me = lax.axis_index("ep")
    core = lax.rem(me, 2)
    chip = me // 2
    partner = chip * 2 + (1 - core)

    def at_chip(delta, which):
        return lax.rem(chip + delta + chips, chips) * 2 + which

    def pos_of(way, hops):
        return far_pos if hops == far else 2 * (hops - 1) + way

    def pos_at(delta):
        if delta == 0:
            return own_pos
        if abs(delta) == far:
            return far_pos
        return pos_of(0, delta) if delta > 0 else pos_of(1, -delta)

    def row_at(pos, which):
        return pos * 2 * tok + which * tok

    def w_pair(step):
        slot = lax.rem(step, STREAM_SLOTS)
        return slot

    def w_copies_shared(step):
        slot = w_pair(step)
        col = pl.ds(pl.multiple_of(step * LANES, LANES), LANES)
        return (
            pltpu.make_async_copy(sg_hbm.at[:, col], wbuf.at[slot, :, pl.ds(0, LANES)], w_sem.at[slot, 0]),
            pltpu.make_async_copy(su_hbm.at[:, col], wbuf.at[slot, :, pl.ds(LANES, LANES)], w_sem.at[slot, 1]),
        )

    def w_copies_expert(step):
        slot = w_pair(step)
        rel = step - sh_steps
        exp = rel // ex_steps
        col = pl.ds(pl.multiple_of((rel - exp * ex_steps) * LANES, LANES), LANES)
        return (
            pltpu.make_async_copy(wg_hbm.at[exp, :, col], wbuf.at[slot, :, pl.ds(0, LANES)], w_sem.at[slot, 0]),
            pltpu.make_async_copy(wu_hbm.at[exp, :, col], wbuf.at[slot, :, pl.ds(LANES, LANES)], w_sem.at[slot, 1]),
        )

    def w_start(step):
        @pl.when(step < sh_steps)
        def _():
            for copy in w_copies_shared(step):
                copy.start()

        @pl.when((step >= sh_steps) & (step < w_steps))
        def _():
            for copy in w_copies_expert(step):
                copy.start()

    def d_copy(chunk, which):
        slot = lax.rem(chunk, 2) * d_per + which
        col = pl.ds(pl.multiple_of(chunk * COLS, COLS), COLS)
        if which < n_exp:
            src = wd_hbm.at[which, :, col]
        else:
            src = sd_hbm.at[pl.ds((which - n_exp) * inter, inter), col]
        return pltpu.make_async_copy(src, dbuf.at[slot], d_sem.at[slot])

    def ag_copy(way, hops, u):
        src_row = row_at(own_pos if hops == 1 else pos_of(way, hops - 1), core) + u * half
        dst_row = row_at(pos_of(way, hops), core) + u * half
        return pltpu.make_async_remote_copy(
            src_ref=xbuf.at[pl.ds(src_row, half), :],
            dst_ref=xbuf.at[pl.ds(dst_row, half), :],
            send_sem=ag_send.at[way, hops - 1, u],
            recv_sem=ag_recv.at[way, hops - 1, u],
            device_id={"ep": at_chip(1 if way == 0 else -1, core)},
            device_id_type=MESH,
        )

    def cc_copy(way, hops, u, which):
        pos = own_pos if hops == 0 else pos_of(way, hops)
        rows = pl.ds(row_at(pos, which) + u * half, half)
        return pltpu.make_async_remote_copy(
            src_ref=xbuf.at[rows, :],
            dst_ref=xbuf.at[rows, :],
            send_sem=cc_send.at[way, hops, u],
            recv_sem=cc_recv.at[way, hops, u],
            device_id={"ep": partner},
            device_id_type=MESH,
        )

    def halves(way, hops):
        if hops == far:
            return (way,)
        return (0, 1) if way == 0 else (1, 0)

    def relay(hops, nth):
        for way in (0, 1):
            if nth >= len(halves(way, hops)):
                continue
            u = halves(way, hops)[nth]
            ag_copy(way, hops, u).wait_recv()
            if hops < far and u in halves(way, hops + 1):
                ag_copy(way, hops + 1, u).start()
            cc_copy(way, hops, u, core).start()

    def gate_copy(delta, other):
        dst_pos = pos_at(delta)
        dest = partner if delta == 0 else at_chip(delta, core if other == 0 else 1 - core)
        return pltpu.make_async_remote_copy(
            src_ref=gsend.at[dest],
            dst_ref=gmsg.at[dst_pos, core],
            send_sem=g_send.at[dst_pos, other],
            recv_sem=g_recv.at[dst_pos, core],
            device_id={"ep": dest},
            device_id_type=MESH,
        )

    deltas = [d for d in range(-(far - 1), far + 1)]

    for step in range(STREAM_SLOTS):
        w_start(jnp.int32(step))
    barrier = pltpu.get_barrier_semaphore()
    for off in range(1, ep_size):
        pl.semaphore_signal(barrier, inc=1, device_id={"ep": lax.rem(me + off, ep_size)}, device_id_type=MESH)

    x_f32 = hidden_ref[...].astype(F32)
    inv_rms = lax.rsqrt(jnp.mean(x_f32 * x_f32, axis=-1, keepdims=True) + NORM_EPS)
    x_norm = (x_f32 * inv_rms * gain_ref[...]).astype(BF16)
    own_row = row_at(own_pos, core)
    xbuf[pl.ds(pl.multiple_of(own_row, tok), tok), :] = x_norm

    pl.semaphore_wait(barrier, ep_size - 1)
    for nth in (0, 1):
        for way in (0, 1):
            ag_copy(way, 1, halves(way, 1)[nth]).start()
    for u in (0, 1):
        cc_copy(0, 0, u, core).start()

    logits = lax.dot_general(
        x_norm.astype(F32),
        router_ref[...],
        (((1,), (1,)), ((), ())),
        precision=lax.Precision.HIGHEST,
        preferred_element_type=F32,
    )
    scores = jax.nn.sigmoid(logits)
    exp_iota = lax.broadcasted_iota(jnp.int32, scores.shape, 1)
    chosen = exp_iota == ids_ref[:, 0:1]
    for k in range(1, top_k):
        chosen = chosen | (exp_iota == ids_ref[:, k : k + 1])
    total = jnp.sum(jnp.where(chosen, scores, 0.0), axis=1, keepdims=True)
    gates = jnp.where(chosen, ROUTE_SCALE * scores / total, -1.0)
    n_all = gates.shape[1]
    gates = jnp.concatenate([gates, jnp.full((tok, LANES - n_all), -1.0, F32)], axis=1)
    gates = jnp.concatenate([gates, jnp.full((LANES - tok, LANES), -1.0, F32)], axis=0)
    gates_t = jnp.transpose(gates)
    for dest in range(ep_size):
        piece = gates_t[dest * n_exp : (dest + 1) * n_exp, :]
        gsend[dest] = jnp.concatenate([piece, jnp.full((8 - n_exp, LANES), -1.0, F32)], axis=0)
    gmsg[own_pos, core] = gsend[me]
    for delta in deltas:
        for other in (0, 1):
            if delta == 0 and other == 0:
                continue
            gate_copy(delta, other).start()

    for chunk in (0, 1):
        for which in range(d_per):
            d_copy(jnp.int32(chunk), which).start()

    def shared_step(step, carry):
        slot = w_pair(step)
        for copy in w_copies_shared(step):
            copy.wait()
        x_own = xbuf[pl.ds(pl.multiple_of(own_row, tok), tok), :]
        both = jnp.dot(x_own, wbuf[slot], preferred_element_type=F32)
        act = (jax.nn.silu(both[:, :LANES]) * both[:, LANES:]).astype(BF16)
        shid[:, pl.ds(pl.multiple_of(step * LANES, LANES), LANES)] = act
        w_start(step + STREAM_SLOTS)
        return carry

    split = sh_steps // 2
    lax.fori_loop(0, split, shared_step, 0)
    relay(1, 0)
    lax.fori_loop(split, sh_steps, shared_step, 0)
    relay(1, 1)

    for delta in deltas:
        for other in (0, 1):
            if delta == 0 and other == 0:
                continue
            if delta == 0:
                src_pos, src_core = own_pos, 1 - core
            else:
                src_pos = pos_at(delta)
                src_core = core if other == 0 else 1 - core
            pltpu.make_async_remote_copy(
                src_ref=gsend.at[0],
                dst_ref=gmsg.at[src_pos, src_core],
                send_sem=g_send.at[src_pos, other],
                recv_sem=g_recv.at[src_pos, src_core],
                device_id={"ep": partner},
                device_id_type=MESH,
            ).wait_recv()

    lane = lax.broadcasted_iota(jnp.int32, (8, LANES), 1)
    packed = []
    for g in range(n_groups):
        b0, b1, b2, b3 = gmsg[2 * g, 0], gmsg[2 * g, 1], gmsg[2 * g + 1, 0], gmsg[2 * g + 1, 1]
        r1 = pltpu.roll(b1, 96, 1)
        r2 = pltpu.roll(b2, 64, 1)
        r3 = pltpu.roll(b3, 32, 1)
        packed.append(jnp.where(lane < 96, b0, r1))
        packed.append(jnp.where(lane < 64, r1, r2))
        packed.append(jnp.where(lane < 32, r2, r3))
    n_tiles = len(packed)
    member = jnp.concatenate([jnp.where(p < 0, 0.0, 1.0) for p in packed], axis=0)
    upper = jnp.where(
        lax.broadcasted_iota(jnp.int32, (LANES, LANES), 0) < lax.broadcasted_iota(jnp.int32, (LANES, LANES), 1), 1.0, 0.0
    ).astype(BF16)
    within = jnp.dot(member.astype(BF16), upper, preferred_element_type=F32)
    base = jnp.zeros((8, 1), F32)
    for t in range(n_tiles):
        m = member[t * 8 : (t + 1) * 8]
        rank = jnp.where(m > 0, within[t * 8 : (t + 1) * 8] + base, -1.0)
        base = base + jnp.sum(m, axis=1, keepdims=True)
        rank_ref[t] = rank
        both = jnp.concatenate([rank, packed[t], jnp.zeros((LANES - 16, LANES), F32)], axis=0)
        cols_ref[t * LANES : (t + 1) * LANES, :] = jnp.transpose(both)

    slot_rows = lax.broadcasted_iota(jnp.int32, (cap, LANES), 0).astype(F32)
    slot_lanes = lax.broadcasted_iota(jnp.int32, (LANES, cap), 1).astype(F32)

    def build(t, carry):
        rank = rank_ref[t]
        col = cols_ref[pl.ds(pl.multiple_of(t * LANES, LANES), LANES), :]
        for e in range(n_exp):
            hot = jnp.where(slot_rows == rank[e : e + 1, :], 1.0, 0.0)
            pick[e * cap : (e + 1) * cap, pl.ds(pl.multiple_of(t * LANES, LANES), LANES)] = hot.astype(BF16)
            hot_t = jnp.where(slot_lanes == col[:, e : e + 1], 1.0, 0.0)
            place[pl.ds(pl.multiple_of(t * LANES, LANES), LANES), e * cap : (e + 1) * cap] = hot_t.astype(BF16)
        return carry

    lax.fori_loop(0, n_tiles, build, 0)

    def gather_group(g):
        def body(n, carry):
            cols = pl.ds(pl.multiple_of(n * COLS, COLS), COLS)
            rows = xbuf[g * group_rows : (g + 1) * group_rows, cols]
            for e in range(n_exp):
                hot = pick[e * cap : (e + 1) * cap, g * group_rows : (g + 1) * group_rows]
                got = jnp.dot(hot, rows, preferred_element_type=F32).astype(BF16)
                if g > 0:
                    got = got + xg[e * cap : (e + 1) * cap, cols]
                xg[e * cap : (e + 1) * cap, cols] = got
            return carry

        lax.fori_loop(0, n_chunks, body, 0)

    def wait_from_core(hops):
        for way in (0, 1):
            if hops == 0 and way == 1:
                continue
            for u in (0, 1) if hops == 0 else halves(way, hops):
                cc_copy(way, hops, u, 1 - core).wait_recv()

    relay(2, 0)
    wait_from_core(1)
    gather_group(0)
    relay(2, 1)
    relay(3, 0)
    wait_from_core(2)
    gather_group(1)
    relay(3, 1)
    wait_from_core(3)
    relay(4, 0)
    gather_group(2)
    wait_from_core(0)
    wait_from_core(4)
    gather_group(3)

    def up_step(step, carry):
        slot = w_pair(step)
        for copy in w_copies_expert(step):
            copy.wait()
        rel = step - sh_steps
        exp = rel // ex_steps
        j = rel - exp * ex_steps
        rows = pl.ds(pl.multiple_of(exp * cap, cap), cap)
        both = jnp.dot(xg[rows, :], wbuf[slot], preferred_element_type=F32)
        act = (jax.nn.silu(both[:, :LANES]) * both[:, LANES:]).astype(BF16)
        hid[rows, pl.ds(pl.multiple_of(j * LANES, LANES), LANES)] = act
        w_start(step + STREAM_SLOTS)
        return carry

    lax.fori_loop(sh_steps, w_steps, up_step, 0)

    def part_copy(chunk):
        par = lax.rem(chunk, 2)
        return pltpu.make_async_remote_copy(
            src_ref=part.at[par, :, 1 - core],
            dst_ref=from_core.at[chunk],
            send_sem=p_send.at[chunk],
            recv_sem=p_recv.at[chunk],
            device_id={"ep": partner},
            device_id_type=MESH,
        )

    def ring_copy(chunk, way, hop):
        dev = {"ep": at_chip(1 if way == 0 else -1, core)}
        if hop == 1:
            src = from_core.at[chunk, far_pos, pl.ds(way * half, half), :]
            dst = ring.at[chunk, way, 0, pl.ds(way * half, half), :]
        else:
            src = ring.at[chunk, way, hop - 2]
            dst = ring.at[chunk, way, hop - 1]
        return pltpu.make_async_remote_copy(
            src_ref=src,
            dst_ref=dst,
            send_sem=r_send.at[chunk, way, hop - 1],
            recv_sem=r_recv.at[chunk, way, hop - 1],
            device_id=dev,
            device_id_type=MESH,
        )

    def dest_pos(way, hops):
        return pos_of(1 - way, hops)

    def compute(chunk):
        par = lax.rem(chunk, 2)
        cols = pl.ds(pl.multiple_of(chunk * COLS, COLS), COLS)
        for e in range(n_exp):
            d_copy(chunk, e).wait()
            got = jnp.dot(hid[e * cap : (e + 1) * cap, :], dbuf[par * d_per + e], preferred_element_type=F32)
            erows[e * cap : (e + 1) * cap, :] = got.astype(BF16)
        for k in range(2):
            d_copy(chunk, n_exp + k).wait()
        shared = jnp.dot(shid[:, :inter], dbuf[par * d_per + n_exp], preferred_element_type=F32)
        shared = shared + jnp.dot(shid[:, inter:], dbuf[par * d_per + n_exp + 1], preferred_element_type=F32)
        sout[:, cols] = shared.astype(BF16)

        @pl.when(chunk + 2 < n_chunks)
        def _():
            for which in range(d_per):
                d_copy(chunk + 2, which).start()

        @pl.when(chunk >= 2)
        def _():
            part_copy(chunk - 2).wait_send()

        def combine(g, carry):
            rows = pl.ds(pl.multiple_of(g * group_rows, group_rows), group_rows)
            acc = None
            for e in range(n_exp):
                got = jnp.dot(
                    place[rows, e * cap : (e + 1) * cap], erows[e * cap : (e + 1) * cap, :], preferred_element_type=F32
                )
                got = cols_ref[rows, 8 + e : 9 + e] * got
                acc = got if acc is None else acc + got
            for b in range(4):
                part[par, 2 * g + b // 2, b % 2] = acc[b * tok : (b + 1) * tok]
            return carry

        lax.fori_loop(0, n_groups, combine, 0)
        part_copy(chunk).start()

    def fold(chunk):
        par = lax.rem(chunk, 2)
        part_copy(chunk).wait_recv()
        for pos in range(chips):
            from_core[chunk, pos] = from_core[chunk, pos] + part[par, pos, core]
        for way in (0, 1):
            ring_copy(chunk, way, 1).start()

    def pass_on(chunk, hop):
        for way in (0, 1):
            ring_copy(chunk, way, hop).wait_recv()
            pos = dest_pos(way, far - hop)
            if hop == 1:
                done = pl.ds(way * half, half)
                rest = pl.ds((1 - way) * half, half)
                ring[chunk, way, 0, done, :] = ring[chunk, way, 0, done, :] + from_core[chunk, pos, done, :]
                ring[chunk, way, 0, rest, :] = from_core[chunk, pos, rest, :]
            else:
                ring[chunk, way, hop - 1] = ring[chunk, way, hop - 1] + from_core[chunk, pos]
            ring_copy(chunk, way, hop + 1).start()

    def finish(chunk):
        cols = pl.ds(pl.multiple_of(chunk * COLS, COLS), COLS)
        for way in (0, 1):
            ring_copy(chunk, way, far).wait_recv()
        routed = from_core[chunk, own_pos] + ring[chunk, 0, far - 1] + ring[chunk, 1, far - 1]
        out_ref[:, cols] = (hidden_ref[:, cols].astype(F32) + sout[:, cols].astype(F32) + routed).astype(BF16)

    def turn(i, carry):
        @pl.when(i < n_chunks)
        def _():
            compute(i)

        @pl.when((i >= far) & (i - far < n_chunks))
        def _():
            finish(i - far)

        for hop in range(far - 1, 0, -1):
            @pl.when((i >= hop) & (i - hop < n_chunks))
            def _():
                pass_on(i - hop, hop)

        @pl.when(i < n_chunks)
        def _():
            fold(i)

        return carry

    lax.fori_loop(0, n_chunks + far, turn, 0)

    for hops in range(1, far + 1):
        for way in (0, 1):
            for u in halves(way, hops):
                ag_copy(way, hops, u).wait_send()
                cc_copy(way, hops, u, core).wait_send()
    for u in (0, 1):
        cc_copy(0, 0, u, core).wait_send()
    for delta in deltas:
        for other in (0, 1):
            if not (delta == 0 and other == 0):
                gate_copy(delta, other).wait_send()

    def drain(chunk, carry):
        @pl.when(chunk >= n_chunks - 2)
        def _():
            part_copy(chunk).wait_send()

        for way in (0, 1):
            for hop in range(1, far + 1):
                ring_copy(chunk, way, hop).wait_send()
        return carry

    lax.fori_loop(0, n_chunks, drain, 0)


def solution(mesh):
    ep_size = mesh.shape["ep"]

    def local_block(hidden_in, norm_gain, router_w, w_gate, w_up, w_down, ws_gate, ws_up, ws_down, expert_ids):
        tok, top_k = expert_ids.shape
        dim = hidden_in.shape[1]
        n_exp, _, inter = w_gate.shape
        s_inter = ws_gate.shape[1]
        chips = ep_size // 2
        far = chips // 2
        n_chunks = dim // COLS
        pair_cap = GROUPS * ((top_k + GROUP_LIMIT - 1) // GROUP_LIMIT) * tok // ep_size
        cap = pair_cap * ep_size // n_exp
        all_tok = ep_size * tok
        slots = n_exp * cap
        n_tiles = all_tok // LANES
        vmem = pl.BlockSpec(memory_space=pltpu.VMEM)
        hbm = pl.BlockSpec(memory_space=pl.ANY)
        dma = pltpu.SemaphoreType.DMA
        return pl.pallas_call(
            functools.partial(moe_kernel, ep_size, cap),
            out_shape=jax.ShapeDtypeStruct((tok, dim), BF16),
            in_specs=[vmem] * 4 + [hbm] * 6,
            out_specs=vmem,
            scratch_shapes=[
                pltpu.VMEM((all_tok, dim), BF16),
                pltpu.VMEM((ep_size, 8, LANES), F32),
                pltpu.VMEM((chips, 2, 8, LANES), F32),
                pltpu.VMEM((n_tiles, 8, LANES), F32),
                pltpu.VMEM((all_tok, LANES), F32),
                pltpu.VMEM((slots, all_tok), BF16),
                pltpu.VMEM((all_tok, slots), BF16),
                pltpu.VMEM((slots, dim), BF16),
                pltpu.VMEM((slots, inter), BF16),
                pltpu.VMEM((tok, s_inter), BF16),
                pltpu.VMEM((tok, dim), BF16),
                pltpu.VMEM((STREAM_SLOTS, dim, 2 * LANES), BF16),
                pltpu.VMEM((2 * (n_exp + 2), inter, COLS), BF16),
                pltpu.VMEM((2, chips, 2, tok, COLS), F32),
                pltpu.VMEM((slots, COLS), BF16),
                pltpu.VMEM((n_chunks, chips, tok, COLS), F32),
                pltpu.VMEM((n_chunks, 2, far, tok, COLS), F32),
                dma((STREAM_SLOTS, 2)),
                dma((2 * (n_exp + 2),)),
                dma((2, far, 2)),
                dma((2, far, 2)),
                dma((2, far + 1, 2)),
                dma((2, far + 1, 2)),
                dma((chips, 2)),
                dma((chips, 2)),
                dma((n_chunks,)),
                dma((n_chunks,)),
                dma((n_chunks, 2, far)),
                dma((n_chunks, 2, far)),
            ],
            compiler_params=pltpu.CompilerParams(
                collective_id=0, has_side_effects=True, vmem_limit_bytes=67043328
            ),
        )(hidden_in, norm_gain.reshape(1, dim), router_w, expert_ids, w_gate, w_up, w_down, ws_gate, ws_up, ws_down)

    row_spec = P(("dp", "ep"), None)
    in_specs = (row_spec, P(), P(), P("ep"), P("ep"), P("ep"), P(), P(), P(), row_spec)
    return jax.shard_map(local_block, mesh=mesh, in_specs=in_specs, out_specs=row_spec, check_vma=False)
```

time: 459 us -> 170 us (0.37)
  waiting for transfers between devices: 259 us -> 0 us
  Pallas kernels: 0 us -> 167 us
  local copies, waits for them, and re-layouts: 75 us -> 3.17 us
  matrix products: 67.2 us -> 0 us
  other arithmetic: 29.3 us -> 0 us
  starting transfers between devices: 26.2 us -> 0 us
    all_to_all x3 -> x0, waiting for transfers between devices: 259 us -> none  [the longest x1 131 us: local_block(): recv_rows = lax.all_to_all(send_rows, 'ep', 0, 0, tiled=True)]
    pallas_call x0 -> x1, Pallas kernels: none -> 167 us  [local_block(): pl.pallas_call(functools.partial(moe_kernel, ep_size, cap), out_shape=jax...]
    dot_general x5 -> x0, matrix products: 67.2 us -> none  [the longest x1 28 us: expert_stack(): jnp.einsum('eci,eid->ecd', hidden, w_down, preferred_element_type=jnp.flo...]
    gather x10 -> x0, local copies, waits for them, and re-layouts: 56.8 us -> none  [the longest x1 16.5 us: local_block(): jnp.take(expert_out, buf_slot, axis=0, mode='fill', fill_value=0)]
    all_to_all x3 -> x0, starting transfers between devices: 26.2 us -> none  [the longest x1 9.6 us: local_block(): recv_exp = lax.all_to_all(slot_exp, 'ep', 0, 0, tiled=True)]
    select_n x9 -> x0, other arithmetic: 17.8 us -> none  [the longest x2 5.95 us: local_block(): send_rows = jnp.take(x_norm, slot_tok, axis=0, mode='fill', fill_value=0)]
    scatter x3 -> x0, local copies, waits for them, and re-layouts: 14.6 us -> none  [the longest x1 6.36 us: local_block(): jnp.full((recv_cap,), recv_cap, jnp.int32).at[buf_slot]]
    reduce_sum x5 -> x0, other arithmetic: 6.57 us -> none  [the longest x1 5.31 us: local_block(): jnp.sum(gate_vals[:, :, None] * pair_out.astype(jnp.float32), axis=1)]
  transfers between devices with their start and end apart: 3 -> 0, of which waited for: 2 -> 0; matrix products, arithmetic and copies ran while one was open for 9% -> 0% of each run, Pallas kernels for 0% -> 0%
where the time goes in v1:
time: 170 us
  Pallas kernels  167 us (98%)
  local copies, waits for them, and re-layouts  3.17 us (2%)
    pallas_call x1, Pallas kernels, local_block(): pl.pallas_call(functools.partial(moe_kernel, ep_size, cap), out_shape=jax...  167 us

profile of v1, /device:TPU:22, one launch (start us, length us, event | category | flops | bytes accessed | tf_op | source)
XLA Modules:
  0.0 169.7 jit_solution(4465191285371618022)
XLA Ops:
  0.0 1.4 copy.11.ids_ref
  1.4 166.5 %shard_map.100 = bf16[96,2048]{1,0:T(8,128)(2,1)} custom-call(bf16[96,2048]{1,0:T(8,128)(2,1)} %hidden_ref.1, f32[1,2048]{1,0:T(1,128)} %bitcast.1, f32[64,2048]{1,0:T(8,128)} %router_ref.1, s32[96,6]{1,0:T(8,128)} %copy.11.ids_ref, bf16[4,2048,1408]{2,1,0:T(8,128)(2,1)} %wg_hbm.1, bf16[4,2048,1408]{2,1,0:T(8,128)(2,1)} %wu_hbm.1, ...), custom_call_target="tpu_custom_call" | custom-call | tf_op jit(solution)/shard_map/pallas_call | solution.py:543
  168.0 1.8 %copy.13 = bf16[96,2048]{1,0:T(8,128)(2,1)} copy(bf16[96,2048]{1,0:T(8,128)(2,1)} %shard_map.100) | data formatting | bytes 786432

commit v2 on v1

--- a/solution.py
+++ b/solution.py
@@ -13,7 +13,8 @@
 GROUP_LIMIT = 4
 LANES = 128
 COLS = 256
-STREAM_SLOTS = 6
+STREAM_SLOTS = 8
+STEP_UNITS = 4
 MESH = pl.DeviceIdType.MESH
 F32 = jnp.float32
 BF16 = jnp.bfloat16
@@ -65,13 +66,13 @@
 ):
     tok, dim = hidden_ref.shape
     half = tok // 2
-    top_k = ids_ref.shape[1]
+    top_k = ids_ref.shape[0]
     n_exp = wg_hbm.shape[0]
     inter = wg_hbm.shape[2]
     s_inter = sg_hbm.shape[1]
     chips = ep_size // 2
     far = chips // 2
-    own_pos = chips - 2
+    own_pos = 0
     far_pos = chips - 1
     n_groups = chips // 2
     group_rows = 4 * tok
@@ -92,7 +93,7 @@
         return lax.rem(chip + delta + chips, chips) * 2 + which
 
     def pos_of(way, hops):
-        return far_pos if hops == far else 2 * (hops - 1) + way
+        return far_pos if hops == far else 2 * hops - 1 + way
 
     def pos_at(delta):
         if delta == 0:
@@ -211,40 +212,39 @@
     own_row = row_at(own_pos, core)
     xbuf[pl.ds(pl.multiple_of(own_row, tok), tok), :] = x_norm
 
-    pl.semaphore_wait(barrier, ep_size - 1)
+    with jax.named_scope("barrier"):
+        pl.semaphore_wait(barrier, ep_size - 1)
     for nth in (0, 1):
         for way in (0, 1):
             ag_copy(way, 1, halves(way, 1)[nth]).start()
     for u in (0, 1):
         cc_copy(0, 0, u, core).start()
 
-    logits = lax.dot_general(
-        x_norm.astype(F32),
-        router_ref[...],
-        (((1,), (1,)), ((), ())),
-        precision=lax.Precision.HIGHEST,
-        preferred_element_type=F32,
-    )
-    scores = jax.nn.sigmoid(logits)
-    exp_iota = lax.broadcasted_iota(jnp.int32, scores.shape, 1)
-    chosen = exp_iota == ids_ref[:, 0:1]
-    for k in range(1, top_k):
-        chosen = chosen | (exp_iota == ids_ref[:, k : k + 1])
-    total = jnp.sum(jnp.where(chosen, scores, 0.0), axis=1, keepdims=True)
-    gates = jnp.where(chosen, ROUTE_SCALE * scores / total, -1.0)
-    n_all = gates.shape[1]
-    gates = jnp.concatenate([gates, jnp.full((tok, LANES - n_all), -1.0, F32)], axis=1)
-    gates = jnp.concatenate([gates, jnp.full((LANES - tok, LANES), -1.0, F32)], axis=0)
-    gates_t = jnp.transpose(gates)
-    for dest in range(ep_size):
-        piece = gates_t[dest * n_exp : (dest + 1) * n_exp, :]
-        gsend[dest] = jnp.concatenate([piece, jnp.full((8 - n_exp, LANES), -1.0, F32)], axis=0)
-    gmsg[own_pos, core] = gsend[me]
-    for delta in deltas:
-        for other in (0, 1):
-            if delta == 0 and other == 0:
-                continue
-            gate_copy(delta, other).start()
+    with jax.named_scope("gates"):
+        logits = lax.dot_general(
+            router_ref[...],
+            x_norm.astype(F32),
+            (((1,), (1,)), ((), ())),
+            precision=lax.Precision.HIGHEST,
+            preferred_element_type=F32,
+        )
+        scores = jax.nn.sigmoid(logits)
+        exp_iota = lax.broadcasted_iota(jnp.int32, scores.shape, 0)
+        chosen = exp_iota == ids_ref[0:1, :]
+        for k in range(1, top_k):
+            chosen = chosen | (exp_iota == ids_ref[k : k + 1, :])
+        total = jnp.sum(jnp.where(chosen, scores, 0.0), axis=0, keepdims=True)
+        gates = jnp.where(chosen, ROUTE_SCALE * scores / total, -1.0)
+        gates_t = jnp.concatenate([gates, jnp.full((gates.shape[0], LANES - tok), -1.0, F32)], axis=1)
+        for dest in range(ep_size):
+            piece = gates_t[dest * n_exp : (dest + 1) * n_exp, :]
+            gsend[dest] = jnp.concatenate([piece, jnp.full((8 - n_exp, LANES), -1.0, F32)], axis=0)
+        gmsg[own_pos, core] = gsend[me]
+        for delta in deltas:
+            for other in (0, 1):
+                if delta == 0 and other == 0:
+                    continue
+                gate_copy(delta, other).start()
 
     for chunk in (0, 1):
         for which in range(d_per):
@@ -261,11 +261,18 @@
         w_start(step + STREAM_SLOTS)
         return carry
 
-    split = sh_steps // 2
-    lax.fori_loop(0, split, shared_step, 0)
-    relay(1, 0)
-    lax.fori_loop(split, sh_steps, shared_step, 0)
-    relay(1, 1)
+    cut_a = sh_steps * 2 // 5
+    cut_b = sh_steps * 9 // 10
+    with jax.named_scope("shared_a"):
+        lax.fori_loop(0, cut_a, shared_step, 0)
+    with jax.named_scope("relay_1_0"):
+        relay(1, 0)
+    with jax.named_scope("shared_b"):
+        lax.fori_loop(cut_a, cut_b, shared_step, 0)
+    with jax.named_scope("relay_1_1"):
+        relay(1, 1)
+    with jax.named_scope("shared_c"):
+        lax.fori_loop(cut_b, sh_steps, shared_step, 0)
 
     for delta in deltas:
         for other in (0, 1):
@@ -323,21 +330,21 @@
             place[pl.ds(pl.multiple_of(t * LANES, LANES), LANES), e * cap : (e + 1) * cap] = hot_t.astype(BF16)
         return carry
 
-    lax.fori_loop(0, n_tiles, build, 0)
-
-    def gather_group(g):
+    with jax.named_scope("build"):
+        lax.fori_loop(0, n_tiles, build, 0)
+
+    def gather_rows(lo, hi, begin, end):
         def body(n, carry):
-            cols = pl.ds(pl.multiple_of(n * COLS, COLS), COLS)
-            rows = xbuf[g * group_rows : (g + 1) * group_rows, cols]
+            cols = pl.ds(pl.multiple_of(n * 2 * COLS, 2 * COLS), 2 * COLS)
+            rows = xbuf[lo:hi, cols]
             for e in range(n_exp):
-                hot = pick[e * cap : (e + 1) * cap, g * group_rows : (g + 1) * group_rows]
-                got = jnp.dot(hot, rows, preferred_element_type=F32).astype(BF16)
-                if g > 0:
+                got = jnp.dot(pick[e * cap : (e + 1) * cap, lo:hi], rows, preferred_element_type=F32).astype(BF16)
+                if lo > 0:
                     got = got + xg[e * cap : (e + 1) * cap, cols]
                 xg[e * cap : (e + 1) * cap, cols] = got
             return carry
 
-        lax.fori_loop(0, n_chunks, body, 0)
+        lax.fori_loop(begin, end, body, 0)
 
     def wait_from_core(hops):
         for way in (0, 1):
@@ -346,36 +353,62 @@
             for u in (0, 1) if hops == 0 else halves(way, hops):
                 cc_copy(way, hops, u, 1 - core).wait_recv()
 
-    relay(2, 0)
-    wait_from_core(1)
-    gather_group(0)
-    relay(2, 1)
-    relay(3, 0)
-    wait_from_core(2)
-    gather_group(1)
-    relay(3, 1)
-    wait_from_core(3)
-    relay(4, 0)
-    gather_group(2)
-    wait_from_core(0)
-    wait_from_core(4)
-    gather_group(3)
-
-    def up_step(step, carry):
-        slot = w_pair(step)
-        for copy in w_copies_expert(step):
-            copy.wait()
-        rel = step - sh_steps
-        exp = rel // ex_steps
-        j = rel - exp * ex_steps
+    def rows_within(hops):
+        return (2 * tok * (1 + 2 * hops)) // LANES * LANES if hops < far else chips * 2 * tok
+
+    wide = n_chunks // 2
+    mid = wide // 2
+    with jax.named_scope("relay_2_0"):
+        relay(2, 0)
+        wait_from_core(0)
+        wait_from_core(1)
+    with jax.named_scope("gather_1"):
+        gather_rows(0, rows_within(1), 0, mid)
+    with jax.named_scope("relay_2_1"):
+        relay(2, 1)
+    with jax.named_scope("gather_1"):
+        gather_rows(0, rows_within(1), mid, wide)
+    with jax.named_scope("wait_2"):
+        wait_from_core(2)
+    with jax.named_scope("gather_2"):
+        gather_rows(rows_within(1), rows_within(2), 0, mid)
+    with jax.named_scope("relay_3_0"):
+        relay(3, 0)
+    with jax.named_scope("gather_2"):
+        gather_rows(rows_within(1), rows_within(2), mid, wide)
+    with jax.named_scope("relay_3_1"):
+        relay(3, 1)
+    with jax.named_scope("wait_3"):
+        wait_from_core(3)
+    with jax.named_scope("gather_3"):
+        gather_rows(rows_within(2), rows_within(3), 0, mid)
+    with jax.named_scope("relay_4_0"):
+        relay(4, 0)
+    with jax.named_scope("gather_3"):
+        gather_rows(rows_within(2), rows_within(3), mid, wide)
+    with jax.named_scope("wait_4"):
+        wait_from_core(4)
+    with jax.named_scope("gather_4"):
+        gather_rows(rows_within(3), rows_within(4), 0, wide)
+
+    def up_expert(exp, carry):
         rows = pl.ds(pl.multiple_of(exp * cap, cap), cap)
-        both = jnp.dot(xg[rows, :], wbuf[slot], preferred_element_type=F32)
-        act = (jax.nn.silu(both[:, :LANES]) * both[:, LANES:]).astype(BF16)
-        hid[rows, pl.ds(pl.multiple_of(j * LANES, LANES), LANES)] = act
-        w_start(step + STREAM_SLOTS)
+        first = sh_steps + exp * ex_steps
+        for lo in range(0, ex_steps, STEP_UNITS):
+            units = range(lo, min(lo + STEP_UNITS, ex_steps))
+            for j in units:
+                for copy in w_copies_expert(first + j):
+                    copy.wait()
+            for j in units:
+                both = jnp.dot(xg[rows, :], wbuf[w_pair(first + j)], preferred_element_type=F32)
+                act = (jax.nn.silu(both[:, :LANES]) * both[:, LANES:]).astype(BF16)
+                hid[rows, j * LANES : (j + 1) * LANES] = act
+            for j in units:
+                w_start(first + j + STREAM_SLOTS)
         return carry
 
-    lax.fori_loop(sh_steps, w_steps, up_step, 0)
+    with jax.named_scope("up"):
+        lax.fori_loop(0, n_exp, up_expert, 0)
 
     def part_copy(chunk):
         par = lax.rem(chunk, 2)
@@ -411,27 +444,21 @@
     def compute(chunk):
         par = lax.rem(chunk, 2)
         cols = pl.ds(pl.multiple_of(chunk * COLS, COLS), COLS)
+        for which in range(d_per):
+            d_copy(chunk, which).wait()
+
+        @pl.when(chunk >= 2)
+        def _():
+            part_copy(chunk - 2).wait_send()
+
         for e in range(n_exp):
-            d_copy(chunk, e).wait()
             got = jnp.dot(hid[e * cap : (e + 1) * cap, :], dbuf[par * d_per + e], preferred_element_type=F32)
             erows[e * cap : (e + 1) * cap, :] = got.astype(BF16)
-        for k in range(2):
-            d_copy(chunk, n_exp + k).wait()
         shared = jnp.dot(shid[:, :inter], dbuf[par * d_per + n_exp], preferred_element_type=F32)
         shared = shared + jnp.dot(shid[:, inter:], dbuf[par * d_per + n_exp + 1], preferred_element_type=F32)
         sout[:, cols] = shared.astype(BF16)
-
-        @pl.when(chunk + 2 < n_chunks)
-        def _():
-            for which in range(d_per):
-                d_copy(chunk + 2, which).start()
-
-        @pl.when(chunk >= 2)
-        def _():
-            part_copy(chunk - 2).wait_send()
-
-        def combine(g, carry):
-            rows = pl.ds(pl.multiple_of(g * group_rows, group_rows), group_rows)
+        for g in range(n_groups):
+            rows = slice(g * group_rows, (g + 1) * group_rows)
             acc = None
             for e in range(n_exp):
                 got = jnp.dot(
@@ -441,9 +468,12 @@
                 acc = got if acc is None else acc + got
             for b in range(4):
                 part[par, 2 * g + b // 2, b % 2] = acc[b * tok : (b + 1) * tok]
-            return carry
-
-        lax.fori_loop(0, n_groups, combine, 0)
+
+        @pl.when(chunk + 2 < n_chunks)
+        def _():
+            for which in range(d_per):
+                d_copy(chunk + 2, which).start()
+
         part_copy(chunk).start()
 
     def fold(chunk):
@@ -477,20 +507,24 @@
     def turn(i, carry):
         @pl.when(i < n_chunks)
         def _():
-            compute(i)
+            with jax.named_scope("compute"):
+                compute(i)
 
         @pl.when((i >= far) & (i - far < n_chunks))
         def _():
-            finish(i - far)
+            with jax.named_scope("finish"):
+                finish(i - far)
 
         for hop in range(far - 1, 0, -1):
             @pl.when((i >= hop) & (i - hop < n_chunks))
             def _():
-                pass_on(i - hop, hop)
+                with jax.named_scope("pass_on"):
+                    pass_on(i - hop, hop)
 
         @pl.when(i < n_chunks)
         def _():
-            fold(i)
+            with jax.named_scope("fold"):
+                fold(i)
 
         return carry
 
@@ -579,7 +613,7 @@
             compiler_params=pltpu.CompilerParams(
                 collective_id=0, has_side_effects=True, vmem_limit_bytes=67043328
             ),
-        )(hidden_in, norm_gain.reshape(1, dim), router_w, expert_ids, w_gate, w_up, w_down, ws_gate, ws_up, ws_down)
+        )(hidden_in, norm_gain.reshape(1, dim), router_w, expert_ids.T, w_gate, w_up, w_down, ws_gate, ws_up, ws_down)
 
     row_spec = P(("dp", "ep"), None)
     in_specs = (row_spec, P(), P(), P("ep"), P("ep"), P("ep"), P(), P(), P(), row_spec)

time: 170 us -> 149 us (0.88)
  Pallas kernels: 167 us -> 147 us
    pallas_call x1, Pallas kernels: 167 us -> 147 us  [local_block(): pl.pallas_call(functools.partial(moe_kernel, ep_size, cap), out_shape=jax...]
where the time goes in v2:
time: 149 us
  Pallas kernels  147 us (99%)
  local copies, waits for them, and re-layouts  1.77 us (1%)
    pallas_call x1, Pallas kernels, local_block(): pl.pallas_call(functools.partial(moe_kernel, ep_size, cap), out_shape=jax...  147 us

profile of v2, /device:TPU:22, one launch (start us, length us, event | category | flops | bytes accessed | tf_op | source)
XLA Modules:
  0.0 148.9 jit_solution(13259454462434065794)
XLA Ops:
  0.0 147.2 %shard_map.100 = bf16[96,2048]{1,0:T(8,128)(2,1)} custom-call(bf16[96,2048]{1,0:T(8,128)(2,1)} %hidden_ref.1, f32[1,2048]{1,0:T(1,128)} %bitcast.2, f32[64,2048]{1,0:T(8,128)} %router_ref.1, s32[6,96]{1,0:T(8,128)} %bitcast.3, bf16[4,2048,1408]{2,1,0:T(8,128)(2,1)} %wg_hbm.1, bf16[4,2048,1408]{2,1,0:T(8,128)(2,1)} %wu_hbm.1, bf16[4,1408,2048]{2,1,0:T(8,128)(2,1)} %wd_hbm.1, ...), custom_call_target="tpu_custom_call" | custom-call | tf_op jit(solution)/shard_map/pallas_call | solution.py:577
  147.2 1.8 %copy.12 = bf16[96,2048]{1,0:T(8,128)(2,1)} copy(bf16[96,2048]{1,0:T(8,128)(2,1)} %shard_map.100) | data formatting | bytes 786432

commit v3 on v2

--- a/solution.py
+++ b/solution.py
@@ -23,10 +23,10 @@
 def moe_kernel(
     ep_size,
     cap,
-    hidden_ref,
-    gain_ref,
-    router_ref,
-    ids_ref,
+    hidden_hbm,
+    gain_hbm,
+    router_hbm,
+    ids_hbm,
     wg_hbm,
     wu_hbm,
     wd_hbm,
@@ -63,10 +63,15 @@
     p_recv,
     r_send,
     r_recv,
+    hidden_ref,
+    gain_ref,
+    router_ref,
+    ids_ref,
+    i_sem,
 ):
-    tok, dim = hidden_ref.shape
+    tok, dim = hidden_hbm.shape
     half = tok // 2
-    top_k = ids_ref.shape[0]
+    top_k = ids_hbm.shape[0]
     n_exp = wg_hbm.shape[0]
     inter = wg_hbm.shape[2]
     s_inter = sg_hbm.shape[1]
@@ -200,11 +205,19 @@
 
     deltas = [d for d in range(-(far - 1), far + 1)]
 
-    for step in range(STREAM_SLOTS):
-        w_start(jnp.int32(step))
     barrier = pltpu.get_barrier_semaphore()
     for off in range(1, ep_size):
         pl.semaphore_signal(barrier, inc=1, device_id={"ep": lax.rem(me + off, ep_size)}, device_id_type=MESH)
+    small = [
+        pltpu.make_async_copy(src, dst, i_sem.at[k])
+        for k, (src, dst) in enumerate(
+            ((hidden_hbm, hidden_ref), (gain_hbm, gain_ref), (ids_hbm, ids_ref), (router_hbm, router_ref))
+        )
+    ]
+    for copy in small:
+        copy.start()
+    small[0].wait()
+    small[1].wait()
 
     x_f32 = hidden_ref[...].astype(F32)
     inv_rms = lax.rsqrt(jnp.mean(x_f32 * x_f32, axis=-1, keepdims=True) + NORM_EPS)
@@ -219,8 +232,12 @@
             ag_copy(way, 1, halves(way, 1)[nth]).start()
     for u in (0, 1):
         cc_copy(0, 0, u, core).start()
+    for step in range(STREAM_SLOTS):
+        w_start(jnp.int32(step))
 
     with jax.named_scope("gates"):
+        small[2].wait()
+        small[3].wait()
         logits = lax.dot_general(
             router_ref[...],
             x_norm.astype(F32),
@@ -410,13 +427,14 @@
     with jax.named_scope("up"):
         lax.fori_loop(0, n_exp, up_expert, 0)
 
-    def part_copy(chunk):
+    def part_copy(chunk, rest):
         par = lax.rem(chunk, 2)
+        which = pl.ds(0, far_pos) if rest else pl.ds(far_pos, 1)
         return pltpu.make_async_remote_copy(
-            src_ref=part.at[par, :, 1 - core],
-            dst_ref=from_core.at[chunk],
-            send_sem=p_send.at[chunk],
-            recv_sem=p_recv.at[chunk],
+            src_ref=part.at[par, which, 1 - core],
+            dst_ref=from_core.at[chunk, which],
+            send_sem=p_send.at[chunk, rest],
+            recv_sem=p_recv.at[chunk, rest],
             device_id={"ep": partner},
             device_id_type=MESH,
         )
@@ -441,23 +459,25 @@
     def dest_pos(way, hops):
         return pos_of(1 - way, hops)
 
-    def compute(chunk):
+    def down(chunk):
         par = lax.rem(chunk, 2)
-        cols = pl.ds(pl.multiple_of(chunk * COLS, COLS), COLS)
         for which in range(d_per):
             d_copy(chunk, which).wait()
-
-        @pl.when(chunk >= 2)
-        def _():
-            part_copy(chunk - 2).wait_send()
-
         for e in range(n_exp):
             got = jnp.dot(hid[e * cap : (e + 1) * cap, :], dbuf[par * d_per + e], preferred_element_type=F32)
             erows[e * cap : (e + 1) * cap, :] = got.astype(BF16)
         shared = jnp.dot(shid[:, :inter], dbuf[par * d_per + n_exp], preferred_element_type=F32)
         shared = shared + jnp.dot(shid[:, inter:], dbuf[par * d_per + n_exp + 1], preferred_element_type=F32)
-        sout[:, cols] = shared.astype(BF16)
-        for g in range(n_groups):
+        sout[:, pl.ds(pl.multiple_of(chunk * COLS, COLS), COLS)] = shared.astype(BF16)
+
+        @pl.when(chunk + 2 < n_chunks)
+        def _():
+            for which in range(d_per):
+                d_copy(chunk + 2, which).start()
+
+    def combine(chunk, groups):
+        par = lax.rem(chunk, 2)
+        for g in groups:
             rows = slice(g * group_rows, (g + 1) * group_rows)
             acc = None
             for e in range(n_exp):
@@ -469,18 +489,16 @@
             for b in range(4):
                 part[par, 2 * g + b // 2, b % 2] = acc[b * tok : (b + 1) * tok]
 
-        @pl.when(chunk + 2 < n_chunks)
-        def _():
-            for which in range(d_per):
-                d_copy(chunk + 2, which).start()
-
-        part_copy(chunk).start()
-
-    def fold(chunk):
+    def fold_rest(chunk):
         par = lax.rem(chunk, 2)
-        part_copy(chunk).wait_recv()
-        for pos in range(chips):
+        part_copy(chunk, 1).wait_recv()
+        for pos in range(far_pos):
             from_core[chunk, pos] = from_core[chunk, pos] + part[par, pos, core]
+
+    def first_hop(chunk):
+        par = lax.rem(chunk, 2)
+        part_copy(chunk, 0).wait_recv()
+        from_core[chunk, far_pos] = from_core[chunk, far_pos] + part[par, far_pos, core]
         for way in (0, 1):
             ring_copy(chunk, way, 1).start()
 
@@ -504,55 +522,77 @@
         routed = from_core[chunk, own_pos] + ring[chunk, 0, far - 1] + ring[chunk, 1, far - 1]
         out_ref[:, cols] = (hidden_ref[:, cols].astype(F32) + sout[:, cols].astype(F32) + routed).astype(BF16)
 
-    def turn(i, carry):
-        @pl.when(i < n_chunks)
+        @pl.when(chunk >= 1)
         def _():
-            with jax.named_scope("compute"):
-                compute(i)
-
-        @pl.when((i >= far) & (i - far < n_chunks))
-        def _():
-            with jax.named_scope("finish"):
-                finish(i - far)
-
-        for hop in range(far - 1, 0, -1):
-            @pl.when((i >= hop) & (i - hop < n_chunks))
-            def _():
-                with jax.named_scope("pass_on"):
-                    pass_on(i - hop, hop)
-
-        @pl.when(i < n_chunks)
-        def _():
-            with jax.named_scope("fold"):
-                fold(i)
-
-        return carry
-
-    lax.fori_loop(0, n_chunks + far, turn, 0)
-
-    for hops in range(1, far + 1):
-        for way in (0, 1):
-            for u in halves(way, hops):
-                ag_copy(way, hops, u).wait_send()
-                cc_copy(way, hops, u, core).wait_send()
-    for u in (0, 1):
-        cc_copy(0, 0, u, core).wait_send()
-    for delta in deltas:
-        for other in (0, 1):
-            if not (delta == 0 and other == 0):
-                gate_copy(delta, other).wait_send()
-
-    def drain(chunk, carry):
-        @pl.when(chunk >= n_chunks - 2)
-        def _():
-            part_copy(chunk).wait_send()
-
+            ring_sends_done(chunk - 1)
+
+    def ring_sends_done(chunk):
         for way in (0, 1):
             for hop in range(1, far + 1):
                 ring_copy(chunk, way, hop).wait_send()
+
+    def gather_sends_done():
+        for hops in range(1, far + 1):
+            for way in (0, 1):
+                for u in halves(way, hops):
+                    ag_copy(way, hops, u).wait_send()
+                    cc_copy(way, hops, u, core).wait_send()
+        for u in (0, 1):
+            cc_copy(0, 0, u, core).wait_send()
+        for delta in deltas:
+            for other in (0, 1):
+                if not (delta == 0 and other == 0):
+                    gate_copy(delta, other).wait_send()
+
+    def turn(i, carry):
+        def for_chunk(lag, name, fn):
+            @pl.when((i >= lag) & (i - lag < n_chunks))
+            def _():
+                with jax.named_scope(name):
+                    fn(i - lag)
+
+        def hops_of(in_middle):
+            for hop in range(1, far + 1):
+                if (hop % 2 == 0) == in_middle:
+                    lag = 3 * hop // 2 if in_middle else (3 * hop - 1) // 2
+                    if hop == far:
+                        for_chunk(lag, "finish", finish)
+                    else:
+                        for_chunk(lag, "pass_on", functools.partial(pass_on, hop=hop))
+
+        for_chunk(0, "down", down)
+        for_chunk(1, "fold_rest", fold_rest)
+        hops_of(True)
+
+        @pl.when(i < n_chunks)
+        def _():
+            @pl.when(i >= 2)
+            def _():
+                for rest in (0, 1):
+                    part_copy(i - 2, rest).wait_send()
+
+            with jax.named_scope("combine_far"):
+                combine(i, (n_groups - 1,))
+                part_copy(i, 0).start()
+            with jax.named_scope("combine"):
+                combine(i, range(n_groups - 1))
+                part_copy(i, 1).start()
+
+        for_chunk(0, "first_hop", first_hop)
+        hops_of(False)
+
+        @pl.when(i == n_chunks)
+        def _():
+            gather_sends_done()
+
         return carry
 
-    lax.fori_loop(0, n_chunks, drain, 0)
+    lax.fori_loop(0, n_chunks + 3 * far // 2, turn, 0)
+
+    for chunk in (n_chunks - 2, n_chunks - 1):
+        for rest in (0, 1):
+            part_copy(jnp.int32(chunk), rest).wait_send()
+    ring_sends_done(jnp.int32(n_chunks - 1))
 
 
 def solution(mesh):
@@ -576,8 +616,8 @@
         dma = pltpu.SemaphoreType.DMA
         return pl.pallas_call(
             functools.partial(moe_kernel, ep_size, cap),
-            out_shape=jax.ShapeDtypeStruct((tok, dim), BF16),
-            in_specs=[vmem] * 4 + [hbm] * 6,
+            out_shape=pltpu.VMEM((tok, dim), BF16),
+            in_specs=[hbm] * 10,
             out_specs=vmem,
             scratch_shapes=[
                 pltpu.VMEM((all_tok, dim), BF16),
@@ -605,13 +645,18 @@
                 dma((2, far + 1, 2)),
                 dma((chips, 2)),
                 dma((chips, 2)),
-                dma((n_chunks,)),
-                dma((n_chunks,)),
+                dma((n_chunks, 2)),
+                dma((n_chunks, 2)),
                 dma((n_chunks, 2, far)),
                 dma((n_chunks, 2, far)),
+                pltpu.VMEM((tok, dim), BF16),
+                pltpu.VMEM((1, dim), F32),
+                pltpu.VMEM(router_w.shape, F32),
+                pltpu.VMEM((top_k, tok), jnp.int32),
+                dma((4,)),
             ],
             compiler_params=pltpu.CompilerParams(
-                collective_id=0, has_side_effects=True, vmem_limit_bytes=67043328
+                collective_id=0, has_side_effects=True, vmem_limit_bytes=66000000
             ),
         )(hidden_in, norm_gain.reshape(1, dim), router_w, expert_ids.T, w_gate, w_up, w_down, ws_gate, ws_up, ws_down)
 

time: 149 us -> 142 us (0.953)
  Pallas kernels: 147 us -> 141 us
    pallas_call x1, Pallas kernels: 147 us -> 141 us  [local_block(): pl.pallas_call(functools.partial(moe_kernel, ep_size, cap), out_shape=plt...]
where the time goes in v3:
time: 142 us
  Pallas kernels  141 us (99%)
    pallas_call x1, Pallas kernels, local_block(): pl.pallas_call(functools.partial(moe_kernel, ep_size, cap), out_shape=plt...  141 us

profile of v3, /device:TPU:22, one launch (start us, length us, event | category | flops | bytes accessed | tf_op | source)
XLA Modules:
  0.0 141.8 jit_solution(3676805475812204925)
XLA Ops:
  0.0 141.0 %shard_map.100 = bf16[96,2048]{1,0:T(8,128)(2,1)S(1)} custom-call(bf16[96,2048]{1,0:T(8,128)(2,1)} %hidden_hbm.1, f32[1,2048]{1,0:T(1,128)} %bitcast.2, f32[64,2048]{1,0:T(8,128)} %router_hbm.1, s32[6,96]{1,0:T(8,128)} %bitcast.3, bf16[4,2048,1408]{2,1,0:T(8,128)(2,1)} %wg_hbm.1, bf16[4,2048,1408]{2,1,0:T(8,128)(2,1)} %wu_hbm.1, ...), custom_call_target="tpu_custom_call" | custom-call | tf_op jit(solution)/shard_map/pallas_call | solution.py:617
  141.0 0.7 copy.12

commit v4 on v3

--- a/solution.py
+++ b/solution.py
@@ -13,8 +13,8 @@
 GROUP_LIMIT = 4
 LANES = 128
 COLS = 256
-STREAM_SLOTS = 8
-STEP_UNITS = 4
+STREAM_SLOTS = 16
+STEP_UNITS = 6
 MESH = pl.DeviceIdType.MESH
 F32 = jnp.float32
 BF16 = jnp.bfloat16
@@ -68,6 +68,8 @@
     router_ref,
     ids_ref,
     i_sem,
+    extra,
+    free_sem,
 ):
     tok, dim = hidden_hbm.shape
     half = tok // 2
@@ -86,7 +88,10 @@
     slots = n_exp * cap
     sh_steps = s_inter // LANES
     ex_steps = inter // LANES
-    w_steps = sh_steps + n_exp * ex_steps
+    depth = dim // 2
+    sh_halves = 2 * sh_steps
+    ex_halves = n_exp * ex_steps
+    w_steps = sh_halves + 2 * ex_halves
     d_per = n_exp + 2
 
     me = lax.axis_index("ep")
@@ -114,31 +119,41 @@
         slot = lax.rem(step, STREAM_SLOTS)
         return slot
 
+    def w_copies(slot, gate, up):
+        return (
+            pltpu.make_async_copy(gate, wbuf.at[slot, :, pl.ds(0, LANES)], w_sem.at[slot]),
+            pltpu.make_async_copy(up, wbuf.at[slot, :, pl.ds(LANES, LANES)], w_sem.at[slot]),
+        )
+
     def w_copies_shared(step):
+        unit = step // 2
+        rows = pl.ds(pl.multiple_of((step - 2 * unit) * depth, depth), depth)
+        col = pl.ds(pl.multiple_of(unit * LANES, LANES), LANES)
+        return w_copies(w_pair(step), sg_hbm.at[rows, col], su_hbm.at[rows, col])
+
+    def w_copies_expert(step):
+        rel = step - sh_halves
+        part_k = rel // ex_halves
+        rel = rel - part_k * ex_halves
+        exp = rel // ex_steps
+        rows = pl.ds(pl.multiple_of(part_k * depth, depth), depth)
+        col = pl.ds(pl.multiple_of((rel - exp * ex_steps) * LANES, LANES), LANES)
+        return w_copies(w_pair(step), wg_hbm.at[exp, rows, col], wu_hbm.at[exp, rows, col])
+
+    def wait_bytes(ref, sem):
+        pltpu.make_async_copy(ref, ref, sem).wait()
+
+    def w_wait(step):
         slot = w_pair(step)
-        col = pl.ds(pl.multiple_of(step * LANES, LANES), LANES)
-        return (
-            pltpu.make_async_copy(sg_hbm.at[:, col], wbuf.at[slot, :, pl.ds(0, LANES)], w_sem.at[slot, 0]),
-            pltpu.make_async_copy(su_hbm.at[:, col], wbuf.at[slot, :, pl.ds(LANES, LANES)], w_sem.at[slot, 1]),
-        )
-
-    def w_copies_expert(step):
-        slot = w_pair(step)
-        rel = step - sh_steps
-        exp = rel // ex_steps
-        col = pl.ds(pl.multiple_of((rel - exp * ex_steps) * LANES, LANES), LANES)
-        return (
-            pltpu.make_async_copy(wg_hbm.at[exp, :, col], wbuf.at[slot, :, pl.ds(0, LANES)], w_sem.at[slot, 0]),
-            pltpu.make_async_copy(wu_hbm.at[exp, :, col], wbuf.at[slot, :, pl.ds(LANES, LANES)], w_sem.at[slot, 1]),
-        )
+        wait_bytes(wbuf.at[slot], w_sem.at[slot])
 
     def w_start(step):
-        @pl.when(step < sh_steps)
+        @pl.when(step < sh_halves)
         def _():
             for copy in w_copies_shared(step):
                 copy.start()
 
-        @pl.when((step >= sh_steps) & (step < w_steps))
+        @pl.when((step >= sh_halves) & (step < w_steps))
         def _():
             for copy in w_copies_expert(step):
                 copy.start()
@@ -152,26 +167,28 @@
             src = sd_hbm.at[pl.ds((which - n_exp) * inter, inter), col]
         return pltpu.make_async_copy(src, dbuf.at[slot], d_sem.at[slot])
 
-    def ag_copy(way, hops, u):
+    def ag_copy(way, hops, k, u):
         src_row = row_at(own_pos if hops == 1 else pos_of(way, hops - 1), core) + u * half
         dst_row = row_at(pos_of(way, hops), core) + u * half
+        cols = pl.ds(k * depth, depth)
         return pltpu.make_async_remote_copy(
-            src_ref=xbuf.at[pl.ds(src_row, half), :],
-            dst_ref=xbuf.at[pl.ds(dst_row, half), :],
-            send_sem=ag_send.at[way, hops - 1, u],
-            recv_sem=ag_recv.at[way, hops - 1, u],
+            src_ref=xbuf.at[pl.ds(src_row, half), cols],
+            dst_ref=xbuf.at[pl.ds(dst_row, half), cols],
+            send_sem=ag_send,
+            recv_sem=ag_recv.at[hops - 1, k, halves(way, hops).index(u)],
             device_id={"ep": at_chip(1 if way == 0 else -1, core)},
             device_id_type=MESH,
         )
 
-    def cc_copy(way, hops, u, which):
+    def cc_copy(way, hops, k, u, which):
         pos = own_pos if hops == 0 else pos_of(way, hops)
         rows = pl.ds(row_at(pos, which) + u * half, half)
+        cols = pl.ds(k * depth, depth)
         return pltpu.make_async_remote_copy(
-            src_ref=xbuf.at[rows, :],
-            dst_ref=xbuf.at[rows, :],
-            send_sem=cc_send.at[way, hops, u],
-            recv_sem=cc_recv.at[way, hops, u],
+            src_ref=xbuf.at[rows, cols],
+            dst_ref=xbuf.at[rows, cols],
+            send_sem=cc_send,
+            recv_sem=cc_recv.at[hops, k],
             device_id={"ep": partner},
             device_id_type=MESH,
         )
@@ -181,15 +198,18 @@
             return (way,)
         return (0, 1) if way == 0 else (1, 0)
 
-    def relay(hops, nth):
+    def send_own(k, nth):
         for way in (0, 1):
-            if nth >= len(halves(way, hops)):
-                continue
-            u = halves(way, hops)[nth]
-            ag_copy(way, hops, u).wait_recv()
-            if hops < far and u in halves(way, hops + 1):
-                ag_copy(way, hops + 1, u).start()
-            cc_copy(way, hops, u, core).start()
+            ag_copy(way, 1, k, halves(way, 1)[nth]).start()
+
+    def relay(hops, k, nth):
+        with jax.named_scope("relay"):
+            wait_bytes(xbuf.at[pl.ds(0, tok), pl.ds(0, depth)], ag_recv.at[hops - 1, k, nth])
+            for way in (0, 1):
+                u = halves(way, hops)[nth]
+                if hops < far and u in halves(way, hops + 1):
+                    ag_copy(way, hops + 1, k, u).start()
+                cc_copy(way, hops, k, u, core).start()
 
     def gate_copy(delta, other):
         dst_pos = pos_at(delta)
@@ -197,8 +217,8 @@
         return pltpu.make_async_remote_copy(
             src_ref=gsend.at[dest],
             dst_ref=gmsg.at[dst_pos, core],
-            send_sem=g_send.at[dst_pos, other],
-            recv_sem=g_recv.at[dst_pos, core],
+            send_sem=g_send,
+            recv_sem=g_recv,
             device_id={"ep": dest},
             device_id_type=MESH,
         )
@@ -228,10 +248,10 @@
     with jax.named_scope("barrier"):
         pl.semaphore_wait(barrier, ep_size - 1)
     for nth in (0, 1):
-        for way in (0, 1):
-            ag_copy(way, 1, halves(way, 1)[nth]).start()
-    for u in (0, 1):
-        cc_copy(0, 0, u, core).start()
+        send_own(0, nth)
+    for k in (0, 1):
+        for u in (0, 1):
+            cc_copy(0, 0, k, u, core).start()
     for step in range(STREAM_SLOTS):
         w_start(jnp.int32(step))
 
@@ -267,47 +287,30 @@
         for which in range(d_per):
             d_copy(jnp.int32(chunk), which).start()
 
-    def shared_step(step, carry):
-        slot = w_pair(step)
-        for copy in w_copies_shared(step):
-            copy.wait()
-        x_own = xbuf[pl.ds(pl.multiple_of(own_row, tok), tok), :]
-        both = jnp.dot(x_own, wbuf[slot], preferred_element_type=F32)
+    def shared_step(unit, carry):
+        steps = (2 * unit, 2 * unit + 1)
+        for step in steps:
+            w_wait(step)
+        rows = pl.ds(pl.multiple_of(own_row, tok), tok)
+        both = jnp.dot(xbuf[rows, :depth], wbuf[w_pair(steps[0])], preferred_element_type=F32)
+        both = both + jnp.dot(xbuf[rows, depth:], wbuf[w_pair(steps[1])], preferred_element_type=F32)
         act = (jax.nn.silu(both[:, :LANES]) * both[:, LANES:]).astype(BF16)
-        shid[:, pl.ds(pl.multiple_of(step * LANES, LANES), LANES)] = act
-        w_start(step + STREAM_SLOTS)
+        shid[:, pl.ds(pl.multiple_of(unit * LANES, LANES), LANES)] = act
+        for step in steps:
+            w_start(step + STREAM_SLOTS)
         return carry
 
-    cut_a = sh_steps * 2 // 5
-    cut_b = sh_steps * 9 // 10
-    with jax.named_scope("shared_a"):
-        lax.fori_loop(0, cut_a, shared_step, 0)
-    with jax.named_scope("relay_1_0"):
-        relay(1, 0)
-    with jax.named_scope("shared_b"):
-        lax.fori_loop(cut_a, cut_b, shared_step, 0)
-    with jax.named_scope("relay_1_1"):
-        relay(1, 1)
-    with jax.named_scope("shared_c"):
-        lax.fori_loop(cut_b, sh_steps, shared_step, 0)
-
-    for delta in deltas:
-        for other in (0, 1):
-            if delta == 0 and other == 0:
-                continue
-            if delta == 0:
-                src_pos, src_core = own_pos, 1 - core
-            else:
-                src_pos = pos_at(delta)
-                src_core = core if other == 0 else 1 - core
-            pltpu.make_async_remote_copy(
-                src_ref=gsend.at[0],
-                dst_ref=gmsg.at[src_pos, src_core],
-                send_sem=g_send.at[src_pos, other],
-                recv_sem=g_recv.at[src_pos, src_core],
-                device_id={"ep": partner},
-                device_id_type=MESH,
-            ).wait_recv()
+    def shared_steps(lo, hi):
+        with jax.named_scope("shared"):
+            lax.fori_loop(min(lo, sh_steps), min(hi, sh_steps), shared_step, 0)
+
+    shared_steps(0, 7)
+    relay(1, 0, 0)
+    shared_steps(7, 11)
+    relay(1, 0, 1)
+    send_own(1, 0)
+
+    wait_bytes(gsend.at[pl.ds(0, ep_size - 1)], g_recv)
 
     lane = lax.broadcasted_iota(jnp.int32, (8, LANES), 1)
     packed = []
@@ -347,10 +350,16 @@
             place[pl.ds(pl.multiple_of(t * LANES, LANES), LANES), e * cap : (e + 1) * cap] = hot_t.astype(BF16)
         return carry
 
+    relay(2, 0, 0)
     with jax.named_scope("build"):
         lax.fori_loop(0, n_tiles, build, 0)
-
-    def gather_rows(lo, hi, begin, end):
+    relay(2, 0, 1)
+    send_own(1, 1)
+
+    def gather_rows(k, first, last):
+        lo = 0 if first == 0 else rows_within(first)
+        hi = rows_within(last)
+
         def body(n, carry):
             cols = pl.ds(pl.multiple_of(n * 2 * COLS, 2 * COLS), 2 * COLS)
             rows = xbuf[lo:hi, cols]
@@ -361,71 +370,97 @@
                 xg[e * cap : (e + 1) * cap, cols] = got
             return carry
 
-        lax.fori_loop(begin, end, body, 0)
-
-    def wait_from_core(hops):
-        for way in (0, 1):
-            if hops == 0 and way == 1:
-                continue
-            for u in (0, 1) if hops == 0 else halves(way, hops):
-                cc_copy(way, hops, u, 1 - core).wait_recv()
+        with jax.named_scope("gather"):
+            lax.fori_loop(k * n_chunks // 4, (k + 1) * n_chunks // 4, body, 0)
+
+    def wait_from_core(hops, k):
+        with jax.named_scope("from_core"):
+            n_rows = 2 * tok if 0 < hops < far else tok
+            wait_bytes(xbuf.at[pl.ds(0, n_rows), pl.ds(0, depth)], cc_recv.at[hops, k])
 
     def rows_within(hops):
-        return (2 * tok * (1 + 2 * hops)) // LANES * LANES if hops < far else chips * 2 * tok
-
-    wide = n_chunks // 2
-    mid = wide // 2
-    with jax.named_scope("relay_2_0"):
-        relay(2, 0)
-        wait_from_core(0)
-        wait_from_core(1)
-    with jax.named_scope("gather_1"):
-        gather_rows(0, rows_within(1), 0, mid)
-    with jax.named_scope("relay_2_1"):
-        relay(2, 1)
-    with jax.named_scope("gather_1"):
-        gather_rows(0, rows_within(1), mid, wide)
-    with jax.named_scope("wait_2"):
-        wait_from_core(2)
-    with jax.named_scope("gather_2"):
-        gather_rows(rows_within(1), rows_within(2), 0, mid)
-    with jax.named_scope("relay_3_0"):
-        relay(3, 0)
-    with jax.named_scope("gather_2"):
-        gather_rows(rows_within(1), rows_within(2), mid, wide)
-    with jax.named_scope("relay_3_1"):
-        relay(3, 1)
-    with jax.named_scope("wait_3"):
-        wait_from_core(3)
-    with jax.named_scope("gather_3"):
-        gather_rows(rows_within(2), rows_within(3), 0, mid)
-    with jax.named_scope("relay_4_0"):
-        relay(4, 0)
-    with jax.named_scope("gather_3"):
-        gather_rows(rows_within(2), rows_within(3), mid, wide)
-    with jax.named_scope("wait_4"):
-        wait_from_core(4)
-    with jax.named_scope("gather_4"):
-        gather_rows(rows_within(3), rows_within(4), 0, wide)
-
-    def up_expert(exp, carry):
-        rows = pl.ds(pl.multiple_of(exp * cap, cap), cap)
-        first = sh_steps + exp * ex_steps
-        for lo in range(0, ex_steps, STEP_UNITS):
-            units = range(lo, min(lo + STEP_UNITS, ex_steps))
-            for j in units:
-                for copy in w_copies_expert(first + j):
-                    copy.wait()
-            for j in units:
-                both = jnp.dot(xg[rows, :], wbuf[w_pair(first + j)], preferred_element_type=F32)
-                act = (jax.nn.silu(both[:, :LANES]) * both[:, LANES:]).astype(BF16)
-                hid[rows, j * LANES : (j + 1) * LANES] = act
-            for j in units:
-                w_start(first + j + STREAM_SLOTS)
-        return carry
-
-    with jax.named_scope("up"):
+        return (2 * tok * (1 + 2 * hops)) // COLS * COLS if hops < far else chips * 2 * tok
+
+    def kept(j, exp):
+        if j < 4:
+            return from_core.at[2 * exp + j // 2, pl.ds(4 * (j % 2), 4)]
+        if j < 8:
+            return ring.at[2 * exp + (j - 4) // 2, j % 2]
+        if j < 10:
+            return part.at[j - 8, pl.ds(2 * exp, 2)]
+        return extra.at[exp]
+
+    def up_half(k, between):
+        def up_expert(exp, carry):
+            rows = pl.ds(pl.multiple_of(exp * cap, cap), cap)
+            first = sh_halves + k * ex_halves + exp * ex_steps
+            for lo in range(0, ex_steps, STEP_UNITS):
+                units = range(lo, min(lo + STEP_UNITS, ex_steps))
+                with jax.named_scope("up"):
+                    for j in units:
+                        w_wait(first + j)
+                    for j in units:
+                        both = jnp.dot(
+                            xg[rows, k * depth : (k + 1) * depth], wbuf[w_pair(first + j)], preferred_element_type=F32
+                        )
+                        view = kept(j, exp)
+                        if k == 0:
+                            view[...] = both.reshape(view.shape)
+                        else:
+                            both = both + view[...].reshape(both.shape)
+                            act = (jax.nn.silu(both[:, :LANES]) * both[:, LANES:]).astype(BF16)
+                            hid[rows, j * LANES : (j + 1) * LANES] = act
+                    for j in units:
+                        w_start(first + j + STREAM_SLOTS)
+                for at, events in between.items():
+                    if at[1] == min(lo // STEP_UNITS, 1):
+                        @pl.when(exp == at[0])
+                        def _():
+                            for event in events:
+                                relay(*event)
+            return carry
+
         lax.fori_loop(0, n_exp, up_expert, 0)
+
+    wait_from_core(0, 0)
+    wait_from_core(1, 0)
+    gather_rows(0, 0, 1)
+    wait_from_core(2, 0)
+    gather_rows(0, 1, 2)
+    shared_steps(11, 13)
+    relay(3, 0, 0)
+    relay(1, 1, 0)
+    shared_steps(13, 18)
+    relay(3, 0, 1)
+    shared_steps(18, 20)
+    wait_from_core(3, 0)
+    gather_rows(0, 2, 3)
+    relay(1, 1, 1)
+    shared_steps(20, sh_steps)
+    relay(4, 0, 0)
+    wait_from_core(0, 1)
+    wait_from_core(1, 1)
+    gather_rows(1, 0, 1)
+    wait_from_core(4, 0)
+    relay(2, 1, 0)
+    gather_rows(0, 3, 4)
+    up_half(
+        0,
+        {
+            (0, 0): [(2, 1, 1)],
+            (1, 0): [(3, 1, 0)],
+            (2, 0): [(3, 1, 1)],
+            (3, 0): [(4, 1, 0)],
+        },
+    )
+    for hops in range(2, far + 1):
+        wait_from_core(hops, 1)
+    gather_rows(1, 1, 4)
+    up_half(1, {})
+
+    pl.semaphore_signal(free_sem.at[0], inc=1, device_id={"ep": partner}, device_id_type=MESH)
+    pl.semaphore_signal(free_sem.at[1], inc=1, device_id={"ep": at_chip(-1, core)}, device_id_type=MESH)
+    pl.semaphore_signal(free_sem.at[2], inc=1, device_id={"ep": at_chip(1, core)}, device_id_type=MESH)
 
     def part_copy(chunk, rest):
         par = lax.rem(chunk, 2)
@@ -433,11 +468,15 @@
         return pltpu.make_async_remote_copy(
             src_ref=part.at[par, which, 1 - core],
             dst_ref=from_core.at[chunk, which],
-            send_sem=p_send.at[chunk, rest],
+            send_sem=p_send.at[par],
             recv_sem=p_recv.at[chunk, rest],
             device_id={"ep": partner},
             device_id_type=MESH,
         )
+
+    def part_sent(chunk):
+        par = lax.rem(chunk, 2)
+        wait_bytes(part.at[par, :, 0], p_send.at[par])
 
     def ring_copy(chunk, way, hop):
         dev = {"ep": at_chip(1 if way == 0 else -1, core)}
@@ -450,8 +489,8 @@
         return pltpu.make_async_remote_copy(
             src_ref=src,
             dst_ref=dst,
-            send_sem=r_send.at[chunk, way, hop - 1],
-            recv_sem=r_recv.at[chunk, way, hop - 1],
+            send_sem=r_send.at[chunk],
+            recv_sem=r_recv.at[chunk, hop - 1],
             device_id=dev,
             device_id_type=MESH,
         )
@@ -499,12 +538,21 @@
         par = lax.rem(chunk, 2)
         part_copy(chunk, 0).wait_recv()
         from_core[chunk, far_pos] = from_core[chunk, far_pos] + part[par, far_pos, core]
+
+        @pl.when(chunk == 0)
+        def _():
+            pl.semaphore_wait(free_sem.at[1], 1)
+            pl.semaphore_wait(free_sem.at[2], 1)
+
         for way in (0, 1):
             ring_copy(chunk, way, 1).start()
 
+    def ring_arrived(chunk, hop):
+        wait_bytes(ring.at[chunk, 0, 0] if hop == 1 else ring.at[chunk, :, 0], r_recv.at[chunk, hop - 1])
+
     def pass_on(chunk, hop):
+        ring_arrived(chunk, hop)
         for way in (0, 1):
-            ring_copy(chunk, way, hop).wait_recv()
             pos = dest_pos(way, far - hop)
             if hop == 1:
                 done = pl.ds(way * half, half)
@@ -517,8 +565,7 @@
 
     def finish(chunk):
         cols = pl.ds(pl.multiple_of(chunk * COLS, COLS), COLS)
-        for way in (0, 1):
-            ring_copy(chunk, way, far).wait_recv()
+        ring_arrived(chunk, far)
         routed = from_core[chunk, own_pos] + ring[chunk, 0, far - 1] + ring[chunk, 1, far - 1]
         out_ref[:, cols] = (hidden_ref[:, cols].astype(F32) + sout[:, cols].astype(F32) + routed).astype(BF16)
 
@@ -527,22 +574,12 @@
             ring_sends_done(chunk - 1)
 
     def ring_sends_done(chunk):
-        for way in (0, 1):
-            for hop in range(1, far + 1):
-                ring_copy(chunk, way, hop).wait_send()
+        wait_bytes(from_core.at[chunk, pl.ds(0, 2 * far - 1)], r_send.at[chunk])
 
     def gather_sends_done():
-        for hops in range(1, far + 1):
-            for way in (0, 1):
-                for u in halves(way, hops):
-                    ag_copy(way, hops, u).wait_send()
-                    cc_copy(way, hops, u, core).wait_send()
-        for u in (0, 1):
-            cc_copy(0, 0, u, core).wait_send()
-        for delta in deltas:
-            for other in (0, 1):
-                if not (delta == 0 and other == 0):
-                    gate_copy(delta, other).wait_send()
+        wait_bytes(xbuf.at[pl.ds(0, (chips - 1) * tok), :], ag_send)
+        wait_bytes(xbuf.at[pl.ds(0, chips * tok), :], cc_send)
+        wait_bytes(gsend.at[pl.ds(0, ep_size - 1)], g_send)
 
     def turn(i, carry):
         def for_chunk(lag, name, fn):
@@ -568,11 +605,15 @@
         def _():
             @pl.when(i >= 2)
             def _():
-                for rest in (0, 1):
-                    part_copy(i - 2, rest).wait_send()
+                part_sent(i)
 
             with jax.named_scope("combine_far"):
                 combine(i, (n_groups - 1,))
+
+                @pl.when(i == 0)
+                def _():
+                    pl.semaphore_wait(free_sem.at[0], 1)
+
                 part_copy(i, 0).start()
             with jax.named_scope("combine"):
                 combine(i, range(n_groups - 1))
@@ -589,9 +630,8 @@
 
     lax.fori_loop(0, n_chunks + 3 * far // 2, turn, 0)
 
-    for chunk in (n_chunks - 2, n_chunks - 1):
-        for rest in (0, 1):
-            part_copy(jnp.int32(chunk), rest).wait_send()
+    for par in (0, 1):
+        part_sent(par)
     ring_sends_done(jnp.int32(n_chunks - 1))
 
 
@@ -631,32 +671,34 @@
                 pltpu.VMEM((slots, inter), BF16),
                 pltpu.VMEM((tok, s_inter), BF16),
                 pltpu.VMEM((tok, dim), BF16),
-                pltpu.VMEM((STREAM_SLOTS, dim, 2 * LANES), BF16),
+                pltpu.VMEM((STREAM_SLOTS, dim // 2, 2 * LANES), BF16),
                 pltpu.VMEM((2 * (n_exp + 2), inter, COLS), BF16),
                 pltpu.VMEM((2, chips, 2, tok, COLS), F32),
                 pltpu.VMEM((slots, COLS), BF16),
                 pltpu.VMEM((n_chunks, chips, tok, COLS), F32),
                 pltpu.VMEM((n_chunks, 2, far, tok, COLS), F32),
-                dma((STREAM_SLOTS, 2)),
+                dma((STREAM_SLOTS,)),
                 dma((2 * (n_exp + 2),)),
-                dma((2, far, 2)),
-                dma((2, far, 2)),
-                dma((2, far + 1, 2)),
-                dma((2, far + 1, 2)),
-                dma((chips, 2)),
-                dma((chips, 2)),
+                dma,
+                dma((far, 2, 2)),
+                dma,
+                dma((far + 1, 2)),
+                dma,
+                dma,
+                dma((2,)),
                 dma((n_chunks, 2)),
-                dma((n_chunks, 2)),
-                dma((n_chunks, 2, far)),
-                dma((n_chunks, 2, far)),
+                dma((n_chunks,)),
+                dma((n_chunks, far)),
                 pltpu.VMEM((tok, dim), BF16),
                 pltpu.VMEM((1, dim), F32),
                 pltpu.VMEM(router_w.shape, F32),
                 pltpu.VMEM((top_k, tok), jnp.int32),
                 dma((4,)),
+                pltpu.VMEM((n_exp, cap, COLS), F32),
+                pltpu.SemaphoreType.REGULAR((3,)),
             ],
             compiler_params=pltpu.CompilerParams(
-                collective_id=0, has_side_effects=True, vmem_limit_bytes=66000000
+                collective_id=0, has_side_effects=True, vmem_limit_bytes=66500000
             ),
         )(hidden_in, norm_gain.reshape(1, dim), router_w, expert_ids.T, w_gate, w_up, w_down, ws_gate, ws_up, ws_down)
 

time: 142 us -> 135 us (0.951)
  Pallas kernels: 141 us -> 134 us
    pallas_call x1, Pallas kernels: 141 us -> 134 us  [local_block(): pl.pallas_call(functools.partial(moe_kernel, ep_size, cap), out_shape=plt...]
where the time goes in v4:
time: 135 us
  Pallas kernels  134 us (99%)
    pallas_call x1, Pallas kernels, local_block(): pl.pallas_call(functools.partial(moe_kernel, ep_size, cap), out_shape=plt...  134 us

profile of v4, /device:TPU:22, one launch (start us, length us, event | category | flops | bytes accessed | tf_op | source)
XLA Modules:
  0.0 134.6 jit_solution(7038848000647828539)
XLA Ops:
  0.0 133.8 %shard_map.100 = bf16[96,2048]{1,0:T(8,128)(2,1)S(1)} custom-call(bf16[96,2048]{1,0:T(8,128)(2,1)} %hidden_hbm.1, f32[1,2048]{1,0:T(1,128)} %bitcast.2, f32[64,2048]{1,0:T(8,128)} %router_hbm.1, s32[6,96]{1,0:T(8,128)} %bitcast.3, bf16[4,2048,1408]{2,1,0:T(8,128)(2,1)} %wg_hbm.1, bf16[4,2048,1408]{2,1,0:T(8,128)(2,1)} %wu_hbm.1, ...), custom_call_target="tpu_custom_call" | custom-call | tf_op jit(solution)/shard_map/pallas_call | solution.py:657
  133.8 0.7 copy.12

commit v5 on v4

--- a/solution.py
+++ b/solution.py
@@ -14,7 +14,6 @@
 LANES = 128
 COLS = 256
 STREAM_SLOTS = 16
-STEP_UNITS = 6
 MESH = pl.DeviceIdType.MESH
 F32 = jnp.float32
 BF16 = jnp.bfloat16
@@ -390,37 +389,29 @@
             return part.at[j - 8, pl.ds(2 * exp, 2)]
         return extra.at[exp]
 
-    def up_half(k, between):
-        def up_expert(exp, carry):
-            rows = pl.ds(pl.multiple_of(exp * cap, cap), cap)
-            first = sh_halves + k * ex_halves + exp * ex_steps
-            for lo in range(0, ex_steps, STEP_UNITS):
-                units = range(lo, min(lo + STEP_UNITS, ex_steps))
-                with jax.named_scope("up"):
-                    for j in units:
-                        w_wait(first + j)
-                    for j in units:
-                        both = jnp.dot(
-                            xg[rows, k * depth : (k + 1) * depth], wbuf[w_pair(first + j)], preferred_element_type=F32
-                        )
-                        view = kept(j, exp)
-                        if k == 0:
-                            view[...] = both.reshape(view.shape)
-                        else:
-                            both = both + view[...].reshape(both.shape)
-                            act = (jax.nn.silu(both[:, :LANES]) * both[:, LANES:]).astype(BF16)
-                            hid[rows, j * LANES : (j + 1) * LANES] = act
-                    for j in units:
-                        w_start(first + j + STREAM_SLOTS)
-                for at, events in between.items():
-                    if at[1] == min(lo // STEP_UNITS, 1):
-                        @pl.when(exp == at[0])
-                        def _():
-                            for event in events:
-                                relay(*event)
-            return carry
-
-        lax.fori_loop(0, n_exp, up_expert, 0)
+    def up_first(exp, carry):
+        rows = pl.ds(pl.multiple_of(exp * cap, cap), cap)
+        first = sh_halves + exp * ex_steps
+        with jax.named_scope("up_first"):
+            for j in range(ex_steps):
+                w_wait(first + j)
+            for j in range(ex_steps):
+                slot = w_pair(first + j)
+                both = jnp.dot(xg[rows, :depth], wbuf[slot], preferred_element_type=F32)
+                view = kept(j, exp)
+                view[...] = both.reshape(view.shape)
+                then = exp + (j + STREAM_SLOTS) // ex_steps
+                wrap = then // n_exp
+                then = then - wrap * n_exp
+                deep = pl.ds(pl.multiple_of(wrap * depth, depth), depth)
+                col = pl.ds((j + STREAM_SLOTS) % ex_steps * LANES, LANES)
+                for copy in w_copies(slot, wg_hbm.at[then, deep, col], wu_hbm.at[then, deep, col]):
+                    copy.start()
+        for at, event in enumerate(((2, 1, 1), (3, 1, 0), (3, 1, 1), (4, 1, 0))):
+            @pl.when(exp == at)
+            def _():
+                relay(*event)
+        return carry
 
     wait_from_core(0, 0)
     wait_from_core(1, 0)
@@ -444,19 +435,41 @@
     wait_from_core(4, 0)
     relay(2, 1, 0)
     gather_rows(0, 3, 4)
-    up_half(
-        0,
-        {
-            (0, 0): [(2, 1, 1)],
-            (1, 0): [(3, 1, 0)],
-            (2, 0): [(3, 1, 1)],
-            (3, 0): [(4, 1, 0)],
-        },
-    )
-    for hops in range(2, far + 1):
-        wait_from_core(hops, 1)
-    gather_rows(1, 1, 4)
-    up_half(1, {})
+    lax.fori_loop(0, n_exp, up_first, 0)
+    wait_from_core(2, 1)
+    wait_from_core(3, 1)
+    gather_rows(1, 1, 3)
+    wait_from_core(4, 1)
+    gather_rows(1, 3, 4)
+    def up_rest(exp, refill):
+        rows = pl.ds(pl.multiple_of(exp * cap, cap), cap)
+        first = sh_halves + ex_halves + exp * ex_steps
+        with jax.named_scope("up_rest"):
+            for j in range(ex_steps):
+                w_wait(first + j)
+            for j in range(ex_steps):
+                slot = w_pair(first + j)
+                both = jnp.dot(xg[rows, depth:], wbuf[slot], preferred_element_type=F32)
+                view = kept(j, exp)
+                both = both + view[...].reshape(both.shape)
+                act = (jax.nn.silu(both[:, :LANES]) * both[:, LANES:]).astype(BF16)
+                hid[rows, j * LANES : (j + 1) * LANES] = act
+                low = pl.ds(depth, depth)
+                ahead = (j + STREAM_SLOTS) // ex_steps
+                if ahead <= refill:
+                    col = pl.ds((j + STREAM_SLOTS) % ex_steps * LANES, LANES)
+                    for copy in w_copies(slot, wg_hbm.at[exp + ahead, low, col], wu_hbm.at[exp + ahead, low, col]):
+                        copy.start()
+
+    furthest = (ex_steps - 1 + STREAM_SLOTS) // ex_steps
+
+    def up_rest_step(exp, carry):
+        up_rest(exp, furthest)
+        return carry
+
+    lax.fori_loop(0, n_exp - furthest, up_rest_step, 0)
+    for exp in range(n_exp - furthest, n_exp):
+        up_rest(jnp.int32(exp), n_exp - 1 - exp)
 
     pl.semaphore_signal(free_sem.at[0], inc=1, device_id={"ep": partner}, device_id_type=MESH)
     pl.semaphore_signal(free_sem.at[1], inc=1, device_id={"ep": at_chip(-1, core)}, device_id_type=MESH)

time: 135 us -> 131 us (0.970)
  Pallas kernels: 134 us -> 130 us
    pallas_call x1, Pallas kernels: 134 us -> 130 us  [local_block(): pl.pallas_call(functools.partial(moe_kernel, ep_size, cap), out_shape=plt...]
where the time goes in v5:
time: 131 us
  Pallas kernels  130 us (99%)
    pallas_call x1, Pallas kernels, local_block(): pl.pallas_call(functools.partial(moe_kernel, ep_size, cap), out_shape=plt...  130 us

profile of v5, /device:TPU:22, one launch (start us, length us, event | category | flops | bytes accessed | tf_op | source)
XLA Modules:
  0.0 130.6 jit_solution(15671797359417902927)
XLA Ops:
  0.0 129.9 %shard_map.100 = bf16[96,2048]{1,0:T(8,128)(2,1)S(1)} custom-call(bf16[96,2048]{1,0:T(8,128)(2,1)} %hidden_hbm.1, f32[1,2048]{1,0:T(1,128)} %bitcast.2, f32[64,2048]{1,0:T(8,128)} %router_hbm.1, s32[6,96]{1,0:T(8,128)} %bitcast.3, bf16[4,2048,1408]{2,1,0:T(8,128)(2,1)} %wg_hbm.1, bf16[4,2048,1408]{2,1,0:T(8,128)(2,1)} %wu_hbm.1, ...), custom_call_target="tpu_custom_call" | custom-call | tf_op jit(solution)/shard_map/pallas_call | solution.py:670
  129.9 0.7 copy.12
